TPU v7x, 32 devices: a 4x4x1 block of a 4x4x8 slice. The times are simulated.
32 devices in a mesh: rep: 1 (over z), dp: 32 (over x, y, core).
Axes of the slice: x: 4, y: 4, z: 1, core: 2. Of those that a mesh axis runs over, the one named last changes fastest.
The devices are a block of a 4x4x8 slice.
Arguments:
- x: bfloat16 [32, 2048, 512], P(('rep', 'dp'))
- dy: bfloat16 [32, 2048, 512], P(('rep', 'dp'))
- w_gate: bfloat16 [2, 512, 8192], P(None, 'dp')
- w_up: bfloat16 [2, 512, 8192], P(None, 'dp')
- w_down: bfloat16 [2, 8192, 512], P(None, 'dp')
- m_w_gate: float32 [2, 512, 8192], P(None, 'dp')
- m_w_up: float32 [2, 512, 8192], P(None, 'dp')
- m_w_down: float32 [2, 8192, 512], P(None, 'dp')
- v_w_gate: float32 [2, 512, 8192], P(None, 'dp')
- v_w_up: float32 [2, 512, 8192], P(None, 'dp')
- v_w_down: float32 [2, 8192, 512], P(None, 'dp')
Outputs:
- output 1: bfloat16 [2, 512, 8192], P('rep', 'dp')
- output 2: bfloat16 [2, 512, 8192], P('rep', 'dp')
- output 3: bfloat16 [2, 8192, 512], P('rep', 'dp')
- output 4: float32 [2, 512, 8192], P('rep', 'dp')
- output 5: float32 [2, 512, 8192], P('rep', 'dp')
- output 6: float32 [2, 8192, 512], P('rep', 'dp')
- output 7: float32 [2, 512, 8192], P('rep', 'dp')
- output 8: float32 [2, 512, 8192], P('rep', 'dp')
- output 9: float32 [2, 8192, 512], P('rep', 'dp')
All inputs are finite; a program needn't handle non-finite values.
Results may differ from a plain program's by a relative error of at most 0.022.
Values are sent between devices in bfloat16 or wider.
A program may use at most 768 MiB of HBM per device.

v0:
```python
import jax
import jax.numpy as jnp
from jax import lax
from jax.sharding import PartitionSpec as P

NAMES = ("w_gate", "w_up", "w_down")


def matmul(a, w):
    return jnp.dot(a, w, preferred_element_type=jnp.float32).astype(jnp.bfloat16)


def normed(h):
    wide = h.astype(jnp.float32)
    scale = lax.rsqrt(jnp.mean(wide**2, -1, keepdims=True) + 1e-6)
    return (wide * scale).astype(jnp.bfloat16)


def layer(h, w):
    a = normed(h)
    gate = jnp.dot(a, w["w_gate"], preferred_element_type=jnp.float32)
    up = jnp.dot(a, w["w_up"], preferred_element_type=jnp.float32)
    return h + matmul((jax.nn.silu(gate) * up).astype(jnp.bfloat16), w["w_down"])


def adamw(w, m, v, g):
    m = 0.9 * m + 0.1 * g
    v = 0.95 * v + 0.05 * g * g
    step = m * lax.rsqrt(v + 1e-8) + 0.1 * w
    return (w - 0.02 * step).astype(jnp.bfloat16), m, v


def clipped(gradients, sum_of_squares, count):
    factor = jnp.minimum(1.0, 0.5 * lax.rsqrt(sum_of_squares / count + 1e-30))
    return [g * factor for g in gradients]


def solution(mesh):
    def fetched(weights, number):
        return {name: lax.all_gather(w[number], "dp", axis=0, tiled=True) for name, w in zip(NAMES, weights, strict=True)}

    def step(x, dy, *arrays):
        weights, m, v = (arrays[i : i + 3] for i in (0, 3, 6))
        layers = weights[0].shape[0]
        h, kept = x[0], []
        for number in range(layers):
            kept.append(h)
            h = layer(h, fetched(weights, number))
        by_h, mine = dy[0], [None] * layers
        for number in reversed(range(layers)):
            _, back = jax.vjp(lambda w, h: layer(h, w), fetched(weights, number), kept[number])
            by_w, by_h = back(by_h)
            mine[number] = [lax.psum_scatter(by_w[name], "dp", scatter_dimension=0, tiled=True) for name in NAMES]
        gradients = [jnp.stack([mine[number][i] for number in range(layers)]).astype(jnp.float32) for i in range(3)]
        squares = lax.psum(sum(jnp.sum(g * g) for g in gradients), "dp")
        gradients = clipped(gradients, squares, lax.psum(1, "dp") * sum(g.size for g in gradients))
        new = [adamw(w.astype(jnp.float32), m, v, g) for w, m, v, g in zip(weights, m, v, gradients, strict=True)]
        return tuple(one[which] for which in range(3) for one in new)

    states, cut = P(("rep", "dp"), None, None), P(None, "dp", None)
    return jax.shard_map(
        step,
        mesh=mesh,
        in_specs=(states, states) + (cut,) * 9,
        out_specs=(P("rep", "dp", None),) * 9,
        check_vma=False,
    )
```

profile of v0, /device:TPU:97, one launch (start us, length us, event | category | flops | bytes accessed | tf_op | source)
XLA Modules:
  0.0 1071.5 jit_solution(10854738919848316935)
XLA Ops:
  15.1 2.9 copy.20
  18.6 4.2 copy.21
  22.8 39.5 %all-gather.13.cloned.1.call-done = bf16[1,512,8192]{2,1,0:T(8,128)(2,1)} async-done(((bf16[1,16,8192]{2,1,0:T(8,128)(2,1)}), bf16[1,512,8192]{2,1,0:T(8,128)(2,1)}) %all-gather.13.cloned.1.call-update) | async-done | bytes 8388624 | tf_op jit(solution)/shard_map/all_gather | solution.py:40
  62.3 29.1 %fusion.35 = f32[2048,8192]{1,0:T(8,128)} fusion(bf16[1,512,8192]{2,1,0:T(8,128)(2,1)} %all-gather.13.cloned.1.call-done, bf16[1,2048,512]{1,2,0:T(8,128)(2,1)S(1)} %copy.20, f32[2048]{0:T(1024)S(1)} %add_rsqrt_fusion), kind=kOutput, calls=%fused_computation.45 | convolution fusion | flops 17183014912 | bytes 77602816 | tf_op jit(solution)/shard_map/dot_general | solution.py:21
  91.4 20.5 %all-gather.15.cloned.1.call-done = bf16[1,512,8192]{2,1,0:T(8,128)(2,1)} async-done(((bf16[1,16,8192]{2,1,0:T(8,128)(2,1)}), bf16[1,512,8192]{2,1,0:T(8,128)(2,1)}) %all-gather.15.cloned.1.call-update) | async-done | bytes 8388624 | tf_op jit(solution)/shard_map/all_gather | solution.py:40
  111.8 60.7 %multiply_convert_fusion.1 = (bf16[2048,8192]{1,0:T(8,128)(2,1)}, f32[2048,8192]{1,0:T(8,128)}) fusion(f32[2048,8192]{1,0:T(8,128)} %fusion.35, bf16[1,512,8192]{2,1,0:T(8,128)(2,1)} %all-gather.15.cloned.1.call-done, bf16[1,2048,512]{1,2,0:T(8,128)(2,1)S(1)} %copy.20, f32[2048]{0:T(1024)S(1)} %add_rsqrt_fusion), kind=kOutput, calls=%fused_computation.17 | convolution fusion | flops 17283678208 | bytes 178266112 | tf_op jit(solution)/shard_map/dot_general | solution.py:22
  172.6 25.4 %fusion.41 = (f32[2048]{0:T(1024)S(1)}, bf16[2048,512]{0,1:T(8,128)(2,1)}) fusion(bf16[2048,8192]{1,0:T(8,128)(2,1)} %get-tuple-element.24, bf16[1,8192,512]{2,1,0:T(8,128)(2,1)} %all-gather.17.cloned.1.call-done, bf16[1,2048,512]{1,2,0:T(8,128)(2,1)S(1)} %copy.20), kind=kOutput, calls=%fused_computation.58 | convolution fusion | flops 17185110016 | bytes 46145536 | tf_op jit(solution)/shard_map/dot_general | solution.py:10
  198.0 12.7 %all-gather.21.cloned.1.call-done = bf16[1,8192,512]{2,1,0:T(8,128)(2,1)} async-done(((bf16[1,256,512]{2,1,0:T(8,128)(2,1)}), bf16[1,8192,512]{2,1,0:T(8,128)(2,1)}) %all-gather.21.cloned.1.call-update) | async-done | bytes 8388624 | tf_op jit(solution)/shard_map/all_gather | solution.py:40
  210.8 25.1 %convolution_convert_fusion.1 = bf16[2048,8192]{1,0:T(8,128)(2,1)} fusion(bf16[1,8192,512]{2,1,0:T(8,128)(2,1)} %all-gather.21.cloned.1.call-done, bf16[1,2048,512]{2,1,0:T(8,128)(2,1)} %param.12), kind=kOutput, calls=%fused_computation.25 | convolution fusion | flops 17196646400 | bytes 44040192 | tf_op jit(solution)/shard_map/transpose(jvp())/dot_general | solution.py:10
  235.8 24.3 %all-gather.23.cloned.1.call-done = bf16[1,512,8192]{2,1,0:T(8,128)(2,1)} async-done(((bf16[1,16,8192]{2,1,0:T(8,128)(2,1)}), bf16[1,512,8192]{2,1,0:T(8,128)(2,1)}) %all-gather.23.cloned.1.call-update) | async-done | bytes 8388624 | tf_op jit(solution)/shard_map/all_gather | solution.py:40
  260.1 29.3 %fusion.22 = f32[2048,8192]{1,0:T(8,128)} fusion(bf16[1,512,8192]{2,1,0:T(8,128)(2,1)} %all-gather.23.cloned.1.call-done, bf16[2048,512]{0,1:T(8,128)(2,1)S(1)} %copy-done.2, f32[2048]{0:T(1024)S(1)} %fusion.91), kind=kOutput, calls=%fused_computation.32 | convolution fusion | flops 17183014912 | bytes 77602816 | tf_op jit(solution)/shard_map/jvp()/dot_general | solution.py:22
  289.4 20.1 %all-gather.19.cloned.1.call-done = bf16[1,512,8192]{2,1,0:T(8,128)(2,1)} async-done(((bf16[1,16,8192]{2,1,0:T(8,128)(2,1)}), bf16[1,512,8192]{2,1,0:T(8,128)(2,1)}) %all-gather.19.cloned.1.call-update) | async-done | bytes 8388624 | tf_op jit(solution)/shard_map/all_gather | solution.py:40
  309.5 78.1 %fusion.2 = (bf16[2048,8192]{1,0:T(8,128)(2,1)}, f32[2048,8192]{1,0:T(8,128)}) fusion(f32[2048,8192]{1,0:T(8,128)} %fusion.22, bf16[2048,8192]{1,0:T(8,128)(2,1)} %convolution_convert_fusion.1, bf16[1,512,8192]{2,1,0:T(8,128)(2,1)} %all-gather.19.cloned.1.call-done, bf16[2048,512]{0,1:T(8,128)(2,1)S(1)} %copy-done.2, f32[2048]{0:T(1024)S(1)} %fusion.91), kind=kOutput, calls=%fused_computation.8 | convolution fusion | flops 17384341504 | bytes 211820544 | tf_op jit(solution)/shard_map/jvp()/dot_general | solution.py:21
  387.6 38.7 %fusion.50 = bf16[2048,512]{0,1:T(8,128)(2,1)} fusion(bf16[1,512,8192]{2,1,0:T(8,128)(2,1)} %all-gather.23.cloned.1.call-done, bf16[2048,8192]{1,0:T(8,128)(2,1)} %convolution_convert_fusion.1, f32[2048,8192]{1,0:T(8,128)} %get-tuple-element.29), kind=kOutput, calls=%fused_computation.63 | convolution fusion | flops 17281581056 | bytes 111149056 | tf_op jit(solution)/shard_map/transpose(jvp())/dot_general | solution.py:22
  426.3 26.9 %fusion.43 = (f32[2048]{0:T(1024)S(1)}, bf16[2048,512]{0,1:T(8,128)(2,1)S(1)}) fusion(bf16[2048,512]{0,1:T(8,128)(2,1)S(1)} %copy-done.2, bf16[2048,512]{0,1:T(8,128)(2,1)} %fusion.50, bf16[2048,8192]{1,0:T(8,128)(2,1)} %get-tuple-element.28, bf16[1,512,8192]{2,1,0:T(8,128)(2,1)} %all-gather.19.cloned.1.call-done), kind=kOutput, calls=%fused_computation.60 | convolution fusion | flops 17185110016 | bytes 48242688 | tf_op jit(solution)/shard_map/transpose(jvp())/dot_general | solution.py:21
  453.2 2.7 fusion.59
  455.9 26.7 %convolution_convert_fusion.3 = bf16[8192,512]{1,0:T(8,128)(2,1)} fusion(bf16[2048,8192]{1,0:T(8,128)(2,1)} %get-tuple-element.24, bf16[2048,512]{0,1:T(8,128)(2,1)} %fusion.59), kind=kOutput, calls=%fused_computation.30 | convolution fusion | flops 17184063488 | bytes 44040192 | tf_op jit(solution)/shard_map/transpose(jvp())/dot_general | solution.py:10
  484.2 46.8 %fusion.20 = bf16[8192,512]{1,0:T(8,128)(2,1)} fusion(f32[2048,8192]{1,0:T(8,128)} %fusion.22, bf16[1,2048,512]{2,1,0:T(8,128)(2,1)S(1)} %copy-done.8, f32[2048,8192]{1,0:T(8,128)} %get-tuple-element.29), kind=kOutput, calls=%fused_computation.31 | convolution fusion | flops 17284726784 | bytes 144703488 | tf_op jit(solution)/shard_map/transpose(jvp())/dot_general | solution.py:10
  531.2 25.6 %convolution_convert_fusion = bf16[2048,8192]{1,0:T(8,128)(2,1)} fusion(bf16[2048,512]{0,1:T(8,128)(2,1)} %fusion.59, bf16[1,8192,512]{2,1,0:T(8,128)(2,1)} %all-gather.17.cloned.1.call-done), kind=kOutput, calls=%fused_computation.24 | convolution fusion | flops 17196646400 | bytes 44040192 | tf_op jit(solution)/shard_map/transpose(jvp())/dot_general | solution.py:10
  556.8 37.8 %fusion.19 = bf16[512,8192]{1,0:T(8,128)(2,1)} fusion(bf16[2048,8192]{1,0:T(8,128)(2,1)} %convolution_convert_fusion, f32[2048,8192]{1,0:T(8,128)} %fusion.35, bf16[1,2048,512]{1,2,0:T(8,128)(2,1)S(1)} %copy-done.1, f32[2048]{0:T(1024)S(1)} %copy-done.14), kind=kOutput, calls=%fused_computation.28 | convolution fusion | flops 17287872512 | bytes 111157248 | tf_op jit(solution)/shard_map/transpose(jvp())/dot_general | solution.py:22
  595.3 38.5 %fusion.15 = bf16[512,8192]{1,0:T(8,128)(2,1)} fusion(bf16[2048,8192]{1,0:T(8,128)(2,1)} %convolution_convert_fusion.1, bf16[2048,512]{0,1:T(8,128)(2,1)} %get-tuple-element.27, f32[2048]{0:T(1024)S(1)} %copy-done.11, f32[2048,8192]{1,0:T(8,128)} %get-tuple-element.29), kind=kOutput, calls=%fused_computation.26 | convolution fusion | flops 17287872512 | bytes 111157248 | tf_op jit(solution)/shard_map/transpose(jvp())/dot_general | solution.py:22
  633.9 57.1 %fusion.16 = bf16[512,8192]{1,0:T(8,128)(2,1)} fusion(f32[2048,8192]{1,0:T(8,128)} %fusion.35, f32[2048,8192]{1,0:T(8,128)} %get-tuple-element.25, bf16[2048,8192]{1,0:T(8,128)(2,1)} %convolution_convert_fusion, bf16[1,2048,512]{1,2,0:T(8,128)(2,1)S(1)} %copy-done.1, f32[2048]{0:T(1024)S(1)} %copy-done.14), kind=kOutput, calls=%fused_computation.27 | convolution fusion | flops 17371758592 | bytes 178266112 | tf_op jit(solution)/shard_map/transpose(jvp())/dot_general | solution.py:21
  692.6 25.6 %convolution_convert_fusion.2 = bf16[512,8192]{1,0:T(8,128)(2,1)} fusion(bf16[2048,8192]{1,0:T(8,128)(2,1)} %get-tuple-element.28, bf16[2048,512]{0,1:T(8,128)(2,1)S(1)} %copy-done.3, f32[2048]{0:T(1024)S(1)} %copy-done.12), kind=kOutput, calls=%fused_computation.29 | convolution fusion | flops 17183014912 | bytes 44048384 | tf_op jit(solution)/shard_map/transpose(jvp())/dot_general | solution.py:21
  718.3 2.1 fusion.81
  720.4 20.8 %reduce-scatter.11.cloned.1.call-done = bf16[16,8192]{1,0:T(8,128)(2,1)} async-done(((bf16[512,8192]{1,0:T(8,128)(2,1)}), bf16[16,8192]{1,0:T(8,128)(2,1)}) %reduce-scatter.11.cloned.1.call-update) | async-done | bytes 262160 | tf_op jit(solution)/shard_map/reduce_scatter | solution.py:53
  741.2 87.7 %reduce-scatter.13.cloned.1.call-done = bf16[16,8192]{1,0:T(8,128)(2,1)} async-done(((bf16[512,8192]{1,0:T(8,128)(2,1)}), bf16[16,8192]{1,0:T(8,128)(2,1)}) %reduce-scatter.13.cloned.1.call-update) | async-done | bytes 262160 | tf_op jit(solution)/shard_map/reduce_scatter | solution.py:53
  828.9 1.9 fusion.80
  830.8 86.0 %reduce-scatter.7.cloned.1.call-done = bf16[16,8192]{1,0:T(8,128)(2,1)} async-done(((bf16[512,8192]{1,0:T(8,128)(2,1)}), bf16[16,8192]{1,0:T(8,128)(2,1)}) %reduce-scatter.7.cloned.1.call-update) | async-done | bytes 262160 | tf_op jit(solution)/shard_map/reduce_scatter | solution.py:53
  916.8 87.8 %reduce-scatter.9.cloned.1.call-done = bf16[16,8192]{1,0:T(8,128)(2,1)} async-done(((bf16[512,8192]{1,0:T(8,128)(2,1)}), bf16[16,8192]{1,0:T(8,128)(2,1)}) %reduce-scatter.9.cloned.1.call-update) | async-done | bytes 262160 | tf_op jit(solution)/shard_map/reduce_scatter | solution.py:53
  1008.4 46.5 %psum.7 = f32[]{:T(128)} all-reduce(f32[]{:T(128)S(6)} %add.99), channel_id=1, replica_groups=mesh['rep'=1,'dp'=32] {'dp'}, use_global_device_ids=true, to_apply=%region_12.13 | all-reduce | flops 1 | bytes 8 | tf_op jit(solution)/shard_map/psum | solution.py:55
  1055.6 3.5 fusion.87
  1059.1 5.1 fusion.78
  (69 shorter events, 14.5 us)
Async XLA Ops:
  7.2 55.1 %all-gather.13.cloned.1.call-start = ((), (), s32[]{:S(2)}) async-start(), calls=%async_computation.12 | async-start | bytes 8650752 | tf_op jit(solution)/shard_map/all_gather | solution.py:40
  9.2 102.7 %all-gather.15.cloned.1.call-start = ((), (), s32[]{:S(2)}) async-start(), calls=%async_computation.13 | async-start | bytes 8650752 | tf_op jit(solution)/shard_map/all_gather | solution.py:40
  11.2 161.4 %all-gather.17.cloned.1.call-start = ((), (), s32[]{:S(2)}) async-start(), calls=%async_computation.14 | async-start | bytes 8650752 | tf_op jit(solution)/shard_map/all_gather | solution.py:40
  13.2 197.6 %all-gather.21.cloned.1.call-start = ((), (), s32[]{:S(2)}) async-start(), calls=%async_computation.16 | async-start | bytes 8650752 | tf_op jit(solution)/shard_map/all_gather | solution.py:40
  13.8 246.3 %all-gather.23.cloned.1.call-start = ((), (), s32[]{:S(2)}) async-start(), calls=%async_computation.17 | async-start | bytes 8650752 | tf_op jit(solution)/shard_map/all_gather | solution.py:40
  14.4 295.1 %all-gather.19.cloned.1.call-start = ((), (), s32[]{:S(2)}) async-start(), calls=%async_computation.15 | async-start | bytes 8650752 | tf_op jit(solution)/shard_map/all_gather | solution.py:40
  15.1 703.2 %reduce-scatter.15.cloned.1.call-start = ((), (), s32[]{:S(2)}) async-start(), calls=%async_computation.10 | async-start | bytes 8650752 | tf_op jit(solution)/shard_map/reduce_scatter | solution.py:53
  18.1 154.5 %copy-start = (bf16[1,2048,512]{1,2,0:T(8,128)(2,1)}, bf16[1,2048,512]{1,2,0:T(8,128)(2,1)S(1)}, u32[]{:S(2)}) copy-start(bf16[1,2048,512]{1,2,0:T(8,128)(2,1)S(1)} %copy.20) | copy-start | bytes 6291460
  18.6 93.3 %copy-start.13 = (f32[2048]{0:T(1024)}, f32[2048]{0:T(1024)S(1)}, u32[]{:S(2)}) copy-start(f32[2048]{0:T(1024)S(1)} %add_rsqrt_fusion) | copy-start | bytes 24580
  198.0 37.8 %copy-start.15 = (f32[2048]{0:T(1024)}, f32[2048]{0:T(1024)S(1)}, u32[]{:S(2)}) copy-start(f32[2048]{0:T(1024)S(1)} %get-tuple-element.26) | copy-start | bytes 24580
  198.0 255.2 %copy-start.10 = (f32[2048]{0:T(1024)}, f32[2048]{0:T(1024)S(1)}, u32[]{:S(2)}) copy-start(f32[2048]{0:T(1024)S(1)} %fusion.91) | copy-start | bytes 24580
  198.0 62.1 %copy-start.2 = (bf16[2048,512]{0,1:T(8,128)(2,1)S(1)}, bf16[2048,512]{0,1:T(8,128)(2,1)}, u32[]{:S(2)}) copy-start(bf16[2048,512]{0,1:T(8,128)(2,1)} %get-tuple-element.27) | copy-start | bytes 6291460
  426.3 26.9 %copy-start.16 = (f32[2048]{0:T(1024)S(1)}, f32[2048]{0:T(1024)}, u32[]{:S(2)}) copy-start(f32[2048]{0:T(1024)} %copy-done.15) | copy-start | bytes 24580
  426.3 26.9 %copy-start.4 = (bf16[1,2048,512]{1,2,0:T(8,128)(2,1)S(1)}, bf16[1,2048,512]{1,2,0:T(8,128)(2,1)}, u32[]{:S(2)}) copy-start(bf16[1,2048,512]{1,2,0:T(8,128)(2,1)} %copy.21) | copy-start | bytes 6291460
  482.6 1.6 copy-start.8
  482.7 235.6 %reduce-scatter.17.cloned.1.call-start = ((), (), s32[]{:S(2)}) async-start(), calls=%async_computation.11 | async-start | bytes 8650752 | tf_op jit(solution)/shard_map/reduce_scatter | solution.py:53
  531.1 25.7 %copy-start.1 = (bf16[1,2048,512]{1,2,0:T(8,128)(2,1)S(1)}, bf16[1,2048,512]{1,2,0:T(8,128)(2,1)}, u32[]{:S(2)}) copy-start(bf16[1,2048,512]{1,2,0:T(8,128)(2,1)} %copy-done) | copy-start | bytes 6291460
  531.1 25.7 %copy-start.14 = (f32[2048]{0:T(1024)S(1)}, f32[2048]{0:T(1024)}, u32[]{:S(2)}) copy-start(f32[2048]{0:T(1024)} %copy-done.13) | copy-start | bytes 24580
  531.1 210.1 %reduce-scatter.11.cloned.1.call-start = ((), (), s32[]{:S(2)}) async-start(), calls=%async_computation.8 | async-start | bytes 8650752 | tf_op jit(solution)/shard_map/reduce_scatter | solution.py:53
  594.6 0.7 copy-start.11
  594.6 234.2 %reduce-scatter.13.cloned.1.call-start = ((), (), s32[]{:S(2)}) async-start(), calls=%async_computation.9 | async-start | bytes 8650752 | tf_op jit(solution)/shard_map/reduce_scatter | solution.py:53
  633.9 283.0 %reduce-scatter.7.cloned.1.call-start = ((), (), s32[]{:S(2)}) async-start(), calls=%async_computation.6 | async-start | bytes 8650752 | tf_op jit(solution)/shard_map/reduce_scatter | solution.py:53
  691.0 1.6 copy-start.3
  691.0 1.6 copy-start.12
  691.0 313.5 %reduce-scatter.9.cloned.1.call-start = ((), (), s32[]{:S(2)}) async-start(), calls=%async_computation.7 | async-start | bytes 8650752 | tf_op jit(solution)/shard_map/reduce_scatter | solution.py:53
  718.2 337.4 %copy-start.5 = (bf16[2,256,512]{2,1,0:T(8,128)(2,1)S(1)}, bf16[2,256,512]{2,1,0:T(8,128)(2,1)}, u32[]{:S(2)}) copy-start(bf16[2,256,512]{2,1,0:T(8,128)(2,1)} %param.15) | copy-start | bytes 1572868
  718.2 340.9 %copy-start.6 = (bf16[2,16,8192]{2,1,0:T(8,128)(2,1)S(1)}, bf16[2,16,8192]{2,1,0:T(8,128)(2,1)}, u32[]{:S(2)}) copy-start(bf16[2,16,8192]{2,1,0:T(8,128)(2,1)} %param.13) | copy-start | bytes 1572868
  718.2 340.9 %copy-start.7 = (bf16[2,16,8192]{2,1,0:T(8,128)(2,1)S(1)}, bf16[2,16,8192]{2,1,0:T(8,128)(2,1)}, u32[]{:S(2)}) copy-start(bf16[2,16,8192]{2,1,0:T(8,128)(2,1)} %param.14) | copy-start | bytes 1572868
  718.2 340.9 %copy-start.9 = (f32[2,16,8192]{2,1,0:T(8,128)S(1)}, f32[2,16,8192]{2,1,0:T(8,128)}, u32[]{:S(2)}) copy-start(f32[2,16,8192]{2,1,0:T(8,128)} %param.19) | copy-start | bytes 3145732
Sparse Core Ops, SparseCore 0:
  10.7 51.5 all-gather.12
  64.9 46.8 all-gather.14
  114.5 46.8 all-gather.16
  163.9 46.8 all-gather.20
  213.2 46.8 all-gather.22
  262.6 46.8 all-gather.18
  482.8 82.3 reduce-scatter.14
  568.8 84.3 reduce-scatter.16
  656.7 84.3 reduce-scatter.10
  744.6 84.2 reduce-scatter.12
  832.4 84.3 reduce-scatter.6
  920.2 84.3 reduce-scatter.8
where the time goes:
time: 1080 us; the launch traced here: 1070 us
  matrix products  571 us (53%)
  waiting for transfers between devices  402 us (37%)
  blocking collectives  46.5 us (4%)
  other arithmetic  17.6 us (2%)
  between operations  17.5 us (2%)
  local copies, waits for them, and re-layouts  16.2 us (2%)
    reduce_scatter x6, waiting for transfers between devices, step(): lax.psum_scatter(by_w[name], 'dp', scatter_dimension=0, tiled=True)  282 us
    dot_general x5, matrix products, layer(): gate = jnp.dot(a, w['w_gate'], preferred_element_type=jnp.float32)  217 us
    dot_general x5, matrix products, layer(): up = jnp.dot(a, w['w_up'], preferred_element_type=jnp.float32)  205 us
    dot_general x5, matrix products, matmul(): jnp.dot(a, w, preferred_element_type=jnp.float32).astype(jnp.bfloat16)  150 us
    all_gather x6, waiting for transfers between devices, fetched(): lax.all_gather(w[number], 'dp', axis=0, tiled=True)  117 us
    psum x1, blocking collectives, step(): squares = lax.psum(sum((jnp.sum(g * g) for g in gradients)), 'dp')  46.5 us
  transfers between devices with their start and end apart: 12, of which 9 were waited for; matrix products, arithmetic and copies ran while one was open for 39% of the time, Pallas kernels for 0%

commit v1 on v0

v1 whole, which is shorter than its diff:
```python
import functools
import math

import jax
import jax.numpy as jnp
from jax import lax
from jax.experimental import pallas as pl
from jax.experimental.pallas import tpu as pltpu
from jax.sharding import PartitionSpec as P

F32, BF16 = jnp.float32, jnp.bfloat16
MESH = pl.DeviceIdType.MESH
ANY = pl.BlockSpec(memory_space=pl.ANY)
VMEM_LIMIT = 63 * 1024 * 1024
LANES = 128
SUB_ROWS, SUB_COLS, SLICE = 512, 256, 32


def dot(a, b):
    return jnp.dot(a, b, preferred_element_type=F32)


def dot_t(a, b):
    return lax.dot_general(a, b, (((1,), (1,)), ((), ())), preferred_element_type=F32)


def aligned(start, size):
    return pl.ds(pl.multiple_of(start, size), size)


def normed(h):
    wide = h.astype(F32)
    return (wide * lax.rsqrt(jnp.mean(wide * wide, -1, keepdims=True) + 1e-6)).astype(BF16)


def normed_back(h, by_a):
    wide = h.astype(F32)
    scale = lax.rsqrt(jnp.mean(wide * wide, -1, keepdims=True) + 1e-6)
    inner = jnp.mean(by_a * wide, -1, keepdims=True)
    return (by_a * scale - wide * (scale * scale * scale * inner)).astype(BF16)


class Place:
    def __init__(self, n):
        self.side = math.isqrt(n // 2)
        assert self.side == 4 and self.side * self.side * 2 == n, n
        self.me = lax.axis_index("dp")
        self.k = lax.rem(self.me, 2)
        chip = self.me // 2
        x, y = chip // self.side, lax.rem(chip, self.side)
        self.pa = jnp.where(self.k == 0, x, y)
        self.pb = jnp.where(self.k == 0, y, x)
        self.partner = chip * 2 + 1 - self.k

    def chip(self, a, b):
        a, b = lax.rem(self.pa + a + self.side, self.side), lax.rem(self.pb + b + self.side, self.side)
        return self.at(a, b)

    def at(self, a, b):
        return jnp.where(self.k == 0, a * self.side + b, b * self.side + a)

    def core(self, a, b):
        return self.chip(a, b) * 2 + self.k

    def neighbours(self):
        return self.core(1, 0), self.core(-1, 0), self.core(0, 1), self.core(0, -1), self.partner


def greet(place):
    barrier = pltpu.get_barrier_semaphore()
    for other in place.neighbours():
        pl.semaphore_signal(barrier, inc=1, device_id={"dp": other}, device_id_type=MESH)
    pl.semaphore_wait(barrier, len(place.neighbours()))


def remote(src, dst, send, recv, other):
    return pltpu.make_async_remote_copy(
        src_ref=src, dst_ref=dst, send_sem=send, recv_sem=recv, device_id={"dp": other}, device_id_type=MESH
    )


def gather_tick(place, tau, total, sems, own, buf):
    own_sem, send, recv = sems
    up_a, down_a, up_b, down_b, partner = place.neighbours()
    k, side = place.k, place.side
    half = own.shape[1] // 2
    low, high = pl.ds(0, half), pl.ds(half, half)
    slots = own_sem.shape[0]

    def stage(number, body):
        n = tau - 2 * number
        pl.when((n >= 0) & (n < total))(lambda: body(n, lax.rem(n, slots)))

    def two(n, s, base, src_up, src_down, up, down):
        return (
            remote(src_up, src_up, send.at[s, base], recv.at[s, base], up),
            remote(src_down, src_down, send.at[s, base + 1], recv.at[s, base + 1], down),
        )

    here = place.chip(0, 0)

    def own_copies(n, s):
        src = own.at[n]
        dst = buf.at[n, here, k]
        return (
            remote(src, dst, send.at[s, 0], recv.at[s, 0], up_a),
            remote(src, dst, send.at[s, 1], recv.at[s, 1], down_a),
        )

    def along_a(n, s):
        return two(n, s, 2, buf.at[n, place.chip(-1, 0), k, low], buf.at[n, place.chip(1, 0), k, high], up_a, down_a)

    def along_b(n, s):
        cps = []
        for a in range(side):
            block = buf.at[n, place.chip(a, 0), k]
            cps += two(n, s, 4, block, block, up_b, down_b)
        return cps

    def along_b2(n, s):
        cps = []
        for a in range(side):
            cps += two(n, s, 6, buf.at[n, place.chip(a, -1), k, low], buf.at[n, place.chip(a, 1), k, high], up_b, down_b)
        return cps

    def across(n, s):
        plane = buf.at[n, :, k]
        return remote(plane, plane, send.at[s, 8], recv.at[s, 8], partner)

    def wait_both(n, s, base, size):
        for d in range(2):
            for sem in (send, recv):
                pltpu.make_async_copy(size(n), size(n), sem.at[s, base + d]).wait()

    one = lambda n: buf.at[n, 0, 0]
    one_half = lambda n: buf.at[n, 0, 0, low]
    four = lambda n: buf.at[n, pl.ds(0, side), 0]
    four_half = lambda n: buf.at[n, pl.ds(0, side), 0, low]

    def stage0(n, s):
        for cp in own_copies(n, s):
            cp.start()
        pltpu.make_async_copy(own.at[n], buf.at[n, here, k], own_sem.at[s]).start()

    def stage1(n, s):
        wait_both(n, s, 0, one)
        for cp in along_a(n, s):
            cp.start()
        pltpu.make_async_copy(own.at[n], buf.at[n, here, k], own_sem.at[s]).wait()

    def stage2(n, s):
        wait_both(n, s, 2, one_half)
        for cp in along_b(n, s):
            cp.start()

    def stage3(n, s):
        wait_both(n, s, 4, four)
        for cp in along_b2(n, s):
            cp.start()

    def stage4(n, s):
        wait_both(n, s, 6, four_half)
        across(n, s).start()

    def stage5(n, s):
        across(n, s).wait()

    for number, body in enumerate((stage0, stage1, stage2, stage3, stage4, stage5)):
        stage(number, body)


GATHER_DEPTH = 10


def first_kernel(
    n_dev, x_h, dy_h, wg_h, wu_h, wd_h,
    buf_h, p_h, grad_h, dh_h,
    own, h, a, aT, dy, dyT, acc, pbuf, guv, wdv, wdc, gout, dout,
    own_sem, send, recv, in_sem, gu_sem, wdv_sem, wdc_sem, p_sem, out_sem, dout_sem,
):
    place = Place(n_dev)
    layers, rows_g, ff = wg_h.shape
    rows_d = wd_h.shape[1]
    tokens, d = x_h.shape
    blocks, quarters = 2, 4
    chips = n_dev // 2
    gu = own.shape[2]
    per = gu // LANES
    units = ff // gu
    halves = rows_d // LANES
    per_half = units // halves
    unit_rows = own.shape[1]
    downs = rows_d // unit_rows
    per_down = downs // halves
    assert units == 2 * downs and halves == 2
    total = layers * (units + downs)
    first = units + downs
    slots = pbuf.shape[0]

    def at_gu0(u):
        return 3 * (u // 2) + lax.rem(u, 2)

    def at_d0(q):
        return 3 * q + 2

    def at_gu1(u):
        return first + (per_down + per_half) * (u // per_half) + per_down + lax.rem(u, per_half)

    def at_d1(q):
        return first + (per_down + per_half) * (q // per_down) + lax.rem(q, per_down)

    def own_pieces(layer, u, n):
        half_no, group = u // per_half, lax.rem(u, per_half)
        for j in range(per):
            cols = aligned((group * per + j) * rows_d + half_no * LANES, LANES)
            for w, r in ((wg_h, 0), (wu_h, rows_g)):
                yield pltpu.make_async_copy(
                    w.at[layer, :, cols], own.at[n, pl.ds(r, rows_g), pl.ds(j * LANES, LANES)], in_sem.at[4]
                )

    def own_down(layer, q, n):
        return pltpu.make_async_copy(wd_h.at[layer, aligned(q * unit_rows, unit_rows)], own.at[n], in_sem.at[4])

    loads = [(x_h, h), (dy_h, dy)]
    for i, (src, dst) in enumerate(loads):
        pltpu.make_async_copy(src, dst, in_sem.at[i]).start()
    for layer, at_gu, at_d in ((0, at_gu0, at_d0), (1, at_gu1, at_d1)):

        @pl.loop(0, units)
        def _(u):
            for cp in own_pieces(layer, u, at_gu(u)):
                cp.start()

        @pl.loop(0, downs)
        def _(q):
            own_down(layer, q, at_d(q)).start()

    greet(place)
    pltpu.make_async_copy(own, own, in_sem.at[4]).wait()

    def tick(tau):
        gather_tick(place, tau, total, (own_sem, send, recv), own, buf_h)

    def gu_load(n, slot):
        return pltpu.make_async_copy(buf_h.at[n], guv.at[slot], gu_sem.at[slot])

    def wdv_load(q):
        half_no, part = q // per_down, lax.rem(q, per_down)
        return pltpu.make_async_copy(
            buf_h.at[at_d0(q)], wdv.at[half_no, :, :, aligned(part * unit_rows, unit_rows)], wdv_sem
        )

    def gate_up(slot):
        w = guv[slot].reshape(n_dev, unit_rows, gu)
        return w[:, :rows_g].reshape(d, gu), w[:, rows_g:].reshape(d, gu)

    def p_store(u):
        slot = lax.rem(u, slots)
        return pltpu.make_async_copy(pbuf.at[slot], p_h.at[u], p_sem.at[slot])

    def hidden(u):
        slot = lax.rem(u, 2)
        out = lax.rem(u, slots)
        gu_load(at_gu0(u), slot).wait()

        @pl.when(u >= slots)
        def _():
            p_store(u - slots).wait()

        @pl.loop(0, blocks)
        def _(t):
            tb = tokens // blocks
            wg, wu = gate_up(slot)
            for r in range(0, tb, SUB_ROWS):
                at = a[aligned(t * tb + r, SUB_ROWS)]
                for col in range(0, gu, SUB_COLS):
                    cols = slice(col, col + SUB_COLS)
                    g_all, up_all = dot(at, wg[:, cols]), dot(at, wu[:, cols])
                    for q in range(0, SUB_ROWS, SLICE):
                        g, up = g_all[q : q + SLICE], up_all[q : q + SLICE]
                        pbuf[out, aligned(t * tb + r + q, SLICE), cols] = (g * (1.0 / (1.0 + jnp.exp(-g))) * up).astype(BF16)

        p_store(u).start()

    def down(half_no, t):
        rows = aligned(t * (tokens // quarters), tokens // quarters)
        total_ = None
        for j in range(per_half):
            w = wdv[half_no, pl.ds(j * per // 2, per // 2)].reshape(gu, d)
            term = dot(pbuf[(half_no * per_half + j) % slots, rows], w)
            total_ = term if total_ is None else total_ + term
        if half_no == 0:
            acc[rows] = total_
        else:
            acc[rows] += total_

    for i, (src, dst) in enumerate(loads):
        pltpu.make_async_copy(src, dst, in_sem.at[i]).wait()

    @pl.loop(0, tokens // 256)
    def _(t):
        rows = aligned(t * 256, 256)
        a[rows] = normed(h[rows])
        dyT[:, rows] = dy[rows].astype(F32).T.astype(BF16)

    @pl.loop(0, first + GATHER_DEPTH + 1)
    def _(tau):
        tick(tau)
        done = tau - GATHER_DEPTH
        kind, r = lax.rem(done, 3), done // 3

        @pl.when((done >= 0) & (done < first))
        def _():
            @pl.when(kind < 2)
            def _():
                gu_load(done, kind).start()

            @pl.when(kind == 2)
            def _():
                wdv_load(r).start()

        n = done - 1
        kind_n, r_n = lax.rem(n, 3), n // 3

        @pl.when(n >= 0)
        def _():
            @pl.when(kind_n < 2)
            def _():
                hidden(2 * r_n + kind_n)

            @pl.when(kind_n == 2)
            def _():
                wdv_load(r_n).wait()

                @pl.when((r_n >= per_down) & (r_n < per_down + 2))
                def _():
                    @pl.loop(0, quarters // 2)
                    def _(t):
                        down(0, (r_n - per_down) * (quarters // 2) + t)

    after = first + GATHER_DEPTH + 1

    @pl.loop(0, quarters)
    def _(t):
        tick(after + t)
        down(1, t)

    after += quarters

    def weights_of(u, slot):
        half_no, group = u // per_half, lax.rem(u, per_half)
        yield gu_load(at_gu1(u), slot)
        for part in range(per_down):
            yield pltpu.make_async_copy(
                buf_h.at[at_d1(half_no * per_down + part), aligned(group * (per // 2), per // 2)],
                wdc.at[slot, :, :, pl.ds(part * unit_rows, unit_rows)],
                wdc_sem.at[slot, part],
            )

    for cp in weights_of(jnp.int32(0), jnp.int32(0)):
        cp.start()
    for i in range(slots):
        p_store(units - slots + i).wait()

    @pl.loop(0, tokens // 256)
    def _(t):
        rows = aligned(t * 256, 256)
        h1 = (h[rows].astype(F32) + acc[rows].astype(BF16).astype(F32)).astype(BF16)
        h[rows] = h1
        a1 = normed(h1)
        a[rows] = a1
        aT[:, rows] = a1.astype(F32).T.astype(BF16)
        acc[rows] = jnp.zeros((256, d), F32)

    def body(c, t, now, before, grads):
        backward_body(
            c, t, now, before, grads, blocks, a, aT, dy, dyT, acc,
            pbuf.at[pl.ds(0, 2)], pbuf.at[pl.ds(2, 2)], pbuf.at[pl.ds(4, 2)],
            gate_up, lambda slot: wdc[slot].reshape(gu, d), gout, dout,
        )

    def flush(c):
        slot = lax.rem(c, 2)
        half_no, group = c // per_half, lax.rem(c, per_half)
        yield pltpu.make_async_copy(gout.at[slot], grad_h.at[1, c], out_sem.at[slot])
        for part in range(per_down):
            yield pltpu.make_async_copy(
                dout.at[slot, :, :, pl.ds(part * unit_rows, unit_rows)],
                grad_h.at[1, units + half_no * per_down + part, aligned(group * (per // 2), per // 2)],
                dout_sem.at[slot, part],
            )

    def chunk_ticks(c):
        @pl.when(after + 2 * c < total + GATHER_DEPTH)
        def _():
            tick(after + 2 * c)
            tick(after + 2 * c + 1)

    backward_loop(units, blocks, body, weights_of, flush, chunk_ticks)

    @pl.loop(0, tokens // 256)
    def _(t):
        rows = aligned(t * 256, 256)
        by_a = acc[rows].astype(BF16).astype(F32)
        back = normed_back(h[rows], by_a)
        a[rows] = (dy[rows].astype(F32) + back.astype(F32)).astype(BF16)

    cp = pltpu.make_async_copy(a, dh_h, in_sem.at[0])
    cp.start()
    cp.wait()


def backward_body(c, t, now, before, grads, blocks, a, aT, by, byT, acc, ps, dg, du, gate_up, down, gout, dout):
    slot = lax.rem(c, 2)
    other = 1 - slot
    tokens, d = a.shape
    tb = tokens // blocks
    part = d // blocks
    fill = []

    def states(i):
        slot_b = jnp.where(t == 0, other, slot)
        rows_b = aligned(lax.rem(t + blocks - 1, blocks) * tb + i * (tb // 2), tb // 2)
        wg, wu = gate_up(slot_b)
        acc[rows_b] += dot_t(dg[slot_b, rows_b], wg) + dot_t(du[slot_b, rows_b], wu)

    def weights(i):
        m = aligned(t * part, part)
        if i == 2:
            dout[other, :, :, :, m] = dot(byT[m], ps[other]).T.astype(BF16).reshape(dout.shape[1:4] + (part,))
            return
        rows_g = gout.shape[3] // 2
        chips = part // rows_g // 2
        grad = dot(aT[m], (dg, du)[i][other]).astype(BF16)
        gout[other, aligned(t * chips, chips), :, pl.ds(i * rows_g, rows_g)] = grad.reshape(chips, 2, rows_g, -1)

    if before and acc is not None:
        fill += [functools.partial(states, i) for i in range(2)]
    if grads:
        fill += [functools.partial(weights, i) for i in range(3 if ps is not None else 2)]
    if not now:
        for piece in fill:
            piece()
        return
    wg, wu = gate_up(slot)
    wd = down(slot)
    gu = wg.shape[1]
    tiles = [(r, col) for r in range(0, tb, SUB_ROWS) for col in range(0, gu, SUB_COLS)]
    done = 0
    for i, (r, col) in enumerate(tiles):
        cols = slice(col, col + SUB_COLS)
        rows = aligned(t * tb + r, SUB_ROWS)
        at = a[rows]
        g_all, up_all = dot(at, wg[:, cols]), dot(at, wu[:, cols])
        dp_all = dot_t(by[rows], wd[cols])
        while done < len(fill) * (i + 1) // len(tiles):
            fill[done]()
            done += 1
        for q in range(0, SUB_ROWS, SLICE):
            g, up, dp = g_all[q : q + SLICE], up_all[q : q + SLICE], dp_all[q : q + SLICE].astype(BF16).astype(F32)
            sig = 1.0 / (1.0 + jnp.exp(-g))
            silu = g * sig
            out = aligned(t * tb + r + q, SLICE)
            if ps is not None:
                ps[slot, out, cols] = (silu * up).astype(BF16)
            du[slot, out, cols] = (dp * silu).astype(BF16)
            dg[slot, out, cols] = (dp * up * (sig + silu * (1.0 - sig))).astype(BF16)


def backward_loop(units, blocks, body, weights_of, flush, ticks, each=lambda c, t: None):
    zero = jnp.int32(0)

    def arrive(c):
        for cp in weights_of(c, lax.rem(c, 2)):
            cp.wait()

    def prefetch(c):
        @pl.when(c + 1 < units)
        def _():
            for cp in weights_of(c + 1, lax.rem(c + 1, 2)):
                cp.start()

    def start(c):
        for cp in flush(c):
            cp.start()

    def wait(c):
        for cp in flush(c):
            cp.wait()

    arrive(zero)
    ticks(zero)
    each(zero, zero)
    body(zero, zero, True, False, False)
    prefetch(zero)

    @pl.loop(1, blocks)
    def _(t):
        each(zero, t)
        body(zero, t, True, True, False)

    @pl.loop(1, units)
    def _(c):
        arrive(c)
        ticks(c)
        each(c, zero)
        body(c, zero, True, True, True)
        prefetch(c)
        pl.when(c > 1)(lambda: wait(c - 2))

        @pl.loop(1, blocks)
        def _(t):
            each(c, t)
            body(c, t, True, True, True)

        start(c - 1)

    last = jnp.int32(units)
    each(last, zero)
    body(last, zero, False, True, True)
    wait(last - 2)

    @pl.loop(1, blocks)
    def _(t):
        each(last, t)
        body(last, t, False, False, True)

    start(last - 1)
    wait(last - 1)


SCATTER_STAGES = 7
SCATTER_AT = (0, 1, 3, 5, 7, 9, 11)
SCATTER_DEPTH = SCATTER_AT[-1]
CREDIT = 2


def scatter_tick(place, tau, issued, source, target, refs):
    grad, got0, out1, got1, out2, got2, mid, out3, got3, out4, got4, fin, squares, load_sem, send, recv, fin_sem, credit = refs
    up_a, down_a, up_b, down_b, partner = place.neighbours()
    neighbours = place.neighbours()
    k, side = place.k, place.side
    half = grad.shape[3] // 2
    low, high = pl.ds(0, half), pl.ds(half, half)
    big, small = grad.shape[0], send.shape[0]

    def f(x):
        return x.astype(F32)

    @pl.when(tau >= CREDIT)
    def _():
        for i in range(len(neighbours)):
            pl.semaphore_wait(credit.at[i], 1)

    def load(b, n):
        return pltpu.make_async_copy(source(n), grad.at[b], load_sem.at[b])

    def across(b, s):
        return (remote(grad.at[b, :, 1 - k], got0.at[b], send.at[s, 0], recv.at[s, 0], partner),)

    def pair(out, got, s, base, up, down):
        return (
            remote(out.at[s, 0], got.at[s, 0], send.at[s, base], recv.at[s, base], up),
            remote(out.at[s, 1], got.at[s, 1], send.at[s, base + 1], recv.at[s, base + 1], down),
        )

    def along_b(s):
        return pair(out1, got1, s, 1, up_b, down_b)

    def along_b2(s):
        return pair(out2, got2, s, 3, up_b, down_b)

    def along_a(s):
        return pair(out3, got3, s, 5, up_a, down_a)

    def along_a2(s):
        return pair(out4, got4, s, 7, up_a, down_a)

    def store(s, n):
        return pltpu.make_async_copy(fin.at[s], target(n), fin_sem.at[s])

    def stage0(b, s, n):
        load(b, n).start()

    def stage1(b, s, n):
        load(b, n).wait()
        for cp in across(b, s):
            cp.start()

    def stage2(b, s, n):
        for cp in across(b, s):
            cp.wait()
        for i in range(side):
            chip = place.at(i, lax.rem(place.pb + 2, side))
            total = f(grad[b, chip, k]) + f(got0[b, chip])
            out1[s, 0, i] = total[:half].astype(BF16)
            out1[s, 1, i] = total[half:].astype(BF16)
        for cp in along_b(s):
            cp.start()

    def stage3(b, s, n):
        for cp in along_b(s):
            cp.wait()
        for i in range(side):
            for way, step in ((0, 1), (1, side - 1)):
                chip = place.at(i, lax.rem(place.pb + step, side))
                total = f(grad[b, chip, k]) + f(got0[b, chip])
                whole = pl.ds(half * way, half)
                rest = pl.ds(half * (1 - way), half)
                out2[s, way, i, whole] = (total[half * way : half * way + half] + f(got1[s, way, i])).astype(BF16)
                out2[s, way, i, rest] = total[half * (1 - way) : half * (2 - way)].astype(BF16)
        for cp in along_b2(s):
            cp.start()

    def stage4(b, s, n):
        for cp in along_b2(s):
            cp.wait()
        for i in range(side):
            chip = place.at(i, place.pb)
            mid[b, i] = f(grad[b, chip, k]) + f(got0[b, chip]) + f(got2[s, 0, i]) + f(got2[s, 1, i])
        far = mid[b, lax.rem(place.pa + 2, side)]
        out3[s, 0] = far[:half].astype(BF16)
        out3[s, 1] = far[half:].astype(BF16)
        for cp in along_a(s):
            cp.start()

    def stage5(b, s, n):
        for cp in along_a(s):
            cp.wait()
        for way, step in ((0, 1), (1, side - 1)):
            total = mid[b, lax.rem(place.pa + step, side)]
            whole = pl.ds(half * way, half)
            rest = pl.ds(half * (1 - way), half)
            out4[s, way, whole] = (total[half * way : half * way + half] + f(got3[s, way])).astype(BF16)
            out4[s, way, rest] = total[half * (1 - way) : half * (2 - way)].astype(BF16)
        for cp in along_a2(s):
            cp.start()

    def stage6(b, s, n):
        for cp in along_a2(s):
            cp.wait()
        result = (mid[b, place.pa] + f(got4[s, 0]) + f(got4[s, 1])).astype(BF16)
        fin[s] = result
        squares[...] += f(result) * f(result)
        cp = store(s, n)
        cp.start()
        cp.wait()

    for after, body in zip(SCATTER_AT, (stage0, stage1, stage2, stage3, stage4, stage5, stage6), strict=True):
        began = tau - after
        here, n = issued(began)
        pl.when((began >= 0) & here)(functools.partial(body, lax.rem(began, big), lax.rem(began, small), n))

    for i, (other, seen_as) in enumerate(zip(neighbours, (1, 0, 3, 2, 4), strict=True)):
        pl.semaphore_signal(credit.at[seen_as], inc=1, device_id={"dp": other}, device_id_type=MESH)


def second_kernel(
    n_dev, x_h, by_h, buf_h, p_h, _,
    grads_h, fin_h, total_o,
    a, aT, by, byT, dg, du, guv, wdc, gout, dout, pv,
    grad, got0, out1, got1, out2, got2, mid, out3, got3, out4, got4, fin, squares, mine, theirs,
    in_sem, gu_sem, wdc_sem, p_sem, out_sem, dout_sem,
    load_sem, send, recv, fin_sem, credit, sum_send, sum_recv,
):
    place = Place(n_dev)
    tokens, d = x_h.shape
    units, _, gu = p_h.shape
    per = gu // LANES
    halves = 2
    per_half = units // halves
    unit_rows = grads_h.shape[4]
    downs = grads_h.shape[1] - units
    per_down = downs // halves
    total = units + downs
    blocks = 2

    for i, (src, dst) in enumerate(((x_h, a), (by_h, by))):
        pltpu.make_async_copy(src, dst, in_sem.at[i]).start()
    greet(place)

    def at_gu0(u):
        return 3 * (u // 2) + lax.rem(u, 2)

    def at_d0(q):
        return 3 * q + 2

    def p_load(u):
        slot = lax.rem(u, 2)
        return pltpu.make_async_copy(p_h.at[u], pv.at[slot], p_sem.at[slot])

    p_load(jnp.int32(0)).start()
    for i, (src, dst) in enumerate(((x_h, a), (by_h, by))):
        pltpu.make_async_copy(src, dst, in_sem.at[i]).wait()

    @pl.loop(0, tokens // 256)
    def _(t):
        rows = aligned(t * 256, 256)
        a0 = normed(a[rows])
        a[rows] = a0
        aT[:, rows] = a0.astype(F32).T.astype(BF16)
        byT[:, rows] = by[rows].astype(F32).T.astype(BF16)

    squares[...] = jnp.zeros_like(squares)

    backlog = total + downs

    def issued(tau):
        chunk, t = tau // 4 - units // 4, lax.rem(tau, 4)
        early = tau < units + 8
        n = jnp.where(early, 3 * (tau // 4) + t, 3 * (units // 4 + 2) + 2 * (chunk - 2) + t)
        u = chunk - 2
        made = (t == 3) & (early == False) & (u < units)
        here = jnp.where(early, t != 3, (t < 2) & (n < backlog))
        return here | made, jnp.where(made, backlog + u, n)

    ticks = units + 4 * (units + 2) + SCATTER_DEPTH

    def source_of(n):
        layer1 = n < total
        return layer1, jnp.where(layer1, n, jnp.where(n < backlog, n - total + units, n - backlog))

    refs = (grad, got0, out1, got1, out2, got2, mid, out3, got3, out4, got4, fin, squares, load_sem, send, recv, fin_sem, credit)

    def tick(tau):
        def source(n):
            layer1, i = source_of(n)
            return grads_h.at[layer1.astype(jnp.int32), i]

        def target(n):
            layer1, i = source_of(n)
            return fin_h.at[layer1.astype(jnp.int32), i]

        scatter_tick(place, tau, issued, source, target, refs)

    def gate_up(slot):
        w = guv[slot].reshape(n_dev, unit_rows, gu)
        return w[:, : unit_rows // 2].reshape(d, gu), w[:, unit_rows // 2 :].reshape(d, gu)

    def split(c):
        return c // per_half, lax.rem(c, per_half)

    def weights_of(u, slot):
        half_no, group = split(u)
        yield pltpu.make_async_copy(buf_h.at[at_gu0(u)], guv.at[slot], gu_sem.at[slot])
        for part in range(per_down):
            yield pltpu.make_async_copy(
                buf_h.at[at_d0(half_no * per_down + part), aligned(group * (per // 2), per // 2)],
                wdc.at[slot, :, :, pl.ds(part * unit_rows, unit_rows)],
                wdc_sem.at[slot, part],
            )

    def down_store(c):
        slot = lax.rem(c, 2)
        half_no, group = split(c)
        for part in range(per_down):
            yield pltpu.make_async_copy(
                dout.at[slot, :, :, pl.ds(part * unit_rows, unit_rows)],
                grads_h.at[0, units + half_no * per_down + part, aligned(group * (per // 2), per // 2)],
                dout_sem.at[slot, part],
            )

    def flush(c):
        slot = lax.rem(c, 2)
        yield pltpu.make_async_copy(gout.at[slot], grads_h.at[0, c], out_sem.at[slot])

    for cp in weights_of(jnp.int32(0), jnp.int32(0)):
        cp.start()

    @pl.loop(0, units)
    def _(u):
        slot = lax.rem(u, 2)
        p_load(u).wait()

        @pl.when(u + 1 < units)
        def _():
            p_load(u + 1).start()

        tick(u)

        @pl.when(u > 1)
        def _():
            for cp in down_store(u - 2):
                cp.wait()

        for r in range(0, d, d // 2):
            m = pl.ds(r, d // 2)
            dout[slot, :, :, :, m] = dot(byT[m], pv[slot]).T.astype(BF16).reshape(dout.shape[1:4] + (d // 2,))
        for cp in down_store(u):
            cp.start()

    for u in (units - 2, units - 1):
        for cp in down_store(jnp.int32(u)):
            cp.wait()

    def body(c, t, now, before, grads):
        backward_body(
            c, t, now, before, grads, blocks, a, aT, by, byT, None, None, dg, du,
            gate_up, lambda slot: wdc[slot].reshape(gu, d), gout, None,
        )

    def each(c, t):
        first = units + 4 * c + 2 * t
        tick(first)
        tick(first + 1)

    backward_loop(units, blocks, body, weights_of, flush, lambda c: None, each)

    @pl.loop(units + 4 * (units + 1), ticks)
    def _(tau):
        tick(tau)

    for i in range(len(place.neighbours())):
        pl.semaphore_wait(credit.at[i], CREDIT)

    up_a, down_a, up_b, down_b, partner = place.neighbours()
    others = [partner]
    for p, up, down in ((place.pa, up_a, down_a), (place.pb, up_b, down_b)):
        even = lax.rem(p, 2) == 0
        others += [jnp.where(even, up, down), jnp.where(even, down, up)]
    so_far = jnp.full(mine.shape[1:], jnp.sum(squares[...]), F32)
    for i, other in enumerate(others):
        mine[i] = so_far
        cp = remote(mine.at[i], theirs.at[i], sum_send.at[i], sum_recv.at[i], other)
        cp.start()
        cp.wait()
        so_far = so_far + theirs[i]
    total_o[...] = so_far


def adamw(w, m, v, g):
    m = 0.9 * m + 0.1 * g
    v = 0.95 * v + 0.05 * g * g
    step = m * lax.rsqrt(v + 1e-8) + 0.1 * w
    return (w - 0.02 * step).astype(BF16), m, v


def solution(mesh):
    n_dev = mesh.shape["dp"]

    def step(x, dy, *arrays):
        weights, m, v = (arrays[i : i + 3] for i in (0, 3, 6))
        x, dy = x[0], dy[0]
        w_gate, w_up, w_down = weights
        layers, rows_g, ff = w_gate.shape
        assert layers == 2
        rows_d, d = w_down.shape[1:]
        tokens = x.shape[0]
        chips = n_dev // 2
        halves = rows_d // LANES
        gu = d
        units, unit_rows = ff // gu, 2 * rows_g
        downs = rows_d // unit_rows
        per = gu // LANES
        total = units + downs
        vmem, dma = pltpu.VMEM, pltpu.SemaphoreType.DMA
        shape = jax.ShapeDtypeStruct
        unit = (chips, 2, unit_rows, gu)
        states = (tokens, d)

        buf, p, grads, by = pl.pallas_call(
            functools.partial(first_kernel, n_dev),
            out_shape=(
                shape((layers * total,) + unit, BF16),
                shape((units, tokens, gu), BF16),
                shape((layers, total) + unit, BF16),
                shape(states, BF16),
            ),
            in_specs=[ANY] * 5,
            out_specs=[ANY] * 4,
            scratch_shapes=[
                vmem((layers * total, unit_rows, gu), BF16),
                vmem(states, BF16),
                vmem(states, BF16),
                vmem(states[::-1], BF16),
                vmem(states, BF16),
                vmem(states[::-1], BF16),
                vmem(states, F32),
                vmem((12, tokens, gu), BF16),
                vmem((2,) + unit, BF16),
                vmem((halves, chips, 2, LANES, d), BF16),
                vmem((2, per // 2, 2, LANES, d), BF16),
                vmem((2,) + unit, BF16),
                vmem((2, per // 2, 2, LANES, d), BF16),
                dma((8,)),
                dma((8, 9)),
                dma((8, 9)),
                dma((5,)),
                dma((2,)),
                dma,
                dma((2, downs // halves)),
                dma((12,)),
                dma((2,)),
                dma((2, downs // halves)),
            ],
            compiler_params=pltpu.CompilerParams(collective_id=0, has_side_effects=True, vmem_limit_bytes=VMEM_LIMIT),
            name="forward_backward",
        )(x, dy, w_gate, w_up, w_down)

        big, small, side = 8, 4, math.isqrt(chips)
        half_block, block = (unit_rows // 2, gu), (unit_rows, gu)
        grads, fin, squares = pl.pallas_call(
            functools.partial(second_kernel, n_dev),
            out_shape=(
                shape(grads.shape, BF16),
                shape((layers, total) + block, BF16),
                shape((8, LANES), F32),
            ),
            in_specs=[ANY] * 5,
            out_specs=[ANY, ANY, pl.BlockSpec(memory_space=vmem)],
            scratch_shapes=[
                vmem(states, BF16),
                vmem(states[::-1], BF16),
                vmem(states, BF16),
                vmem(states[::-1], BF16),
                vmem((2, tokens, gu), BF16),
                vmem((2, tokens, gu), BF16),
                vmem((2,) + unit, BF16),
                vmem((2, per // 2, 2, LANES, d), BF16),
                vmem((2,) + unit, BF16),
                vmem((2, per // 2, 2, LANES, d), BF16),
                vmem((2, tokens, gu), BF16),
                vmem((big,) + unit, BF16),
                vmem((big, chips) + block, BF16),
                vmem((small, 2, side) + half_block, BF16),
                vmem((small, 2, side) + half_block, BF16),
                vmem((small, 2, side) + block, BF16),
                vmem((small, 2, side) + block, BF16),
                vmem((big, side) + block, F32),
                vmem((small, 2) + half_block, BF16),
                vmem((small, 2) + half_block, BF16),
                vmem((small, 2) + block, BF16),
                vmem((small, 2) + block, BF16),
                vmem((small,) + block, BF16),
                vmem(block, F32),
                vmem((5, 8, LANES), F32),
                vmem((5, 8, LANES), F32),
                dma((2,)),
                dma((2,)),
                dma((2, downs // halves)),
                dma((2,)),
                dma((2,)),
                dma((2, downs // halves)),
                dma((big,)),
                dma((small, 9)),
                dma((small, 9)),
                dma((small,)),
                pltpu.SemaphoreType.REGULAR((5,)),
                dma((5,)),
                dma((5,)),
            ],
            input_output_aliases={4: 0},
            compiler_params=pltpu.CompilerParams(collective_id=1, has_side_effects=True, vmem_limit_bytes=VMEM_LIMIT),
            name="backward_scatter",
        )(x, by, buf, p, grads)

        pair = fin[:, :units].reshape(layers, halves, units // halves, 2, rows_g, per, LANES)
        pair = pair.transpose(3, 0, 4, 2, 5, 1, 6).reshape(2, layers, rows_g, ff)
        gradients = [pair[0], pair[1], fin[:, units:].reshape(layers, rows_d, d)]
        count = n_dev * sum(g.size for g in gradients)
        factor = jnp.minimum(1.0, 0.5 * lax.rsqrt(squares[0, 0] / count + 1e-30))
        new = [adamw(w.astype(F32), m, v, g.astype(F32) * factor) for w, m, v, g in zip(weights, m, v, gradients, strict=True)]
        return tuple(one[which] for which in range(3) for one in new)

    states, cut = P(("rep", "dp"), None, None), P(None, "dp", None)
    return jax.shard_map(
        step,
        mesh=mesh,
        in_specs=(states, states) + (cut,) * 9,
        out_specs=(P("rep", "dp", None),) * 9,
        check_vma=False,
    )
```

time: 1080 us -> 576 us (0.53)
  matrix products: 571 us -> 0 us
  Pallas kernels: 0 us -> 550 us
  waiting for transfers between devices: 402 us -> 0 us
  blocking collectives: 46.5 us -> 0 us
  between operations: 17.5 us -> 1.94 us
    dot_general x15 -> x0, matrix products: 571 us -> none  [the longest x5 217 us: layer(): gate = jnp.dot(a, w['w_gate'], preferred_element_type=jnp.float32)]
    pallas_call x0 -> x2, Pallas kernels: none -> 550 us  [the longest x1 293 us: step(): pl.pallas_call(functools.partial(first_kernel, n_dev), out_shape=(shape((...]
    reduce_scatter x6 -> x0, waiting for transfers between devices: 282 us -> none  [step(): lax.psum_scatter(by_w[name], 'dp', scatter_dimension=0, tiled=True)]
    all_gather x6 -> x0, waiting for transfers between devices: 117 us -> none  [fetched(): lax.all_gather(w[number], 'dp', axis=0, tiled=True)]
    psum x1 -> x0, blocking collectives: 46.5 us -> none  [step(): squares = lax.psum(sum((jnp.sum(g * g) for g in gradients)), 'dp')]
  transfers between devices with their start and end apart: 12 -> 0, of which waited for: 9 -> 0; matrix products, arithmetic and copies ran while one was open for 39% -> 0% of each run, Pallas kernels for 0% -> 0%
where the time goes in v1:
time: 576 us; the launch traced here: 567 us
  Pallas kernels  550 us (95%)
  other arithmetic  9.23 us (2%)
  local copies, waits for them, and re-layouts  6.09 us (1%)
    pallas_call x1, Pallas kernels, step(): pl.pallas_call(functools.partial(first_kernel, n_dev), out_shape=(shape((...  293 us
    pallas_call x1, Pallas kernels, step(): pl.pallas_call(functools.partial(second_kernel, n_dev), out_shape=(shape(...  256 us

profile of v1, /device:TPU:97, one launch (start us, length us, event | category | flops | bytes accessed | tf_op | source)
XLA Modules:
  0.0 566.9 jit_solution(11348796839531763274)
XLA Ops:
  0.6 293.2 %forward_backward.1 = (bf16[48,16,2,32,512]{4,3,2,1,0:T(8,128)(2,1)}, bf16[16,2048,512]{2,1,0:T(8,128)(2,1)}, bf16[2,24,16,2,32,512]{5,4,3,2,1,0:T(8,128)(2,1)}, bf16[2048,512]{1,0:T(8,128)(2,1)}) custom-call(bf16[2048,512]{1,0:T(8,128)(2,1)} %bitcast.15, bf16[2048,512]{1,0:T(8,128)(2,1)} %bitcast.18, bf16[2,16,8192]{2,1,0:T(8,128)(2,1)} %wg_h.1, ...), custom_call_target="tpu_custom_call" | custom-call | tf_op jit(solution)/shard_map/forward_backward/pallas_call | solution.py:861
  293.9 256.4 %backward_scatter.1 = (bf16[2,24,16,2,32,512]{5,4,3,2,1,0:T(8,128)(2,1)}, bf16[2,24,32,512]{3,2,1,0:T(8,128)(2,1)}, f32[8,128]{1,0:T(8,128)}) custom-call(bf16[2048,512]{1,0:T(8,128)(2,1)} %bitcast.16, bf16[2048,512]{1,0:T(8,128)(2,1)} %get-tuple-element.15.by_h, ...), custom_call_target="tpu_custom_call", output_to_operand_aliasing={{0}: (4, {})} | custom-call | tf_op jit(solution)/shard_map/backward_scatter/pallas_call | solution.py:902
  550.3 0.0 copy-start.2
  550.3 1.3 slice.19
  552.3 2.2 convert_multiply_fusion.3
  554.5 0.0 copy-done.2
  554.5 0.1 slice.17
  554.6 0.5 reshape.43
  555.2 1.2 copy.28
  556.4 0.2 convert_multiply_fusion.4
  556.6 0.6 copy.26
  557.2 0.8 mul.122
  558.0 0.6 copy.25
  558.6 0.8 mul.112
  559.5 0.0 copy-start
  559.5 0.0 copy-start.1
  559.5 0.0 copy-start.3
  559.5 0.0 copy-start.4
  559.5 0.0 copy-start.5
  559.6 0.0 copy-start.6
  559.6 4.0 fusion.8
  563.6 0.0 copy-done
  563.6 0.0 copy-done.1
  563.6 0.0 copy-done.3
  563.6 0.0 copy-done.4
  563.6 0.0 copy-done.5
  563.6 0.0 copy-done.6
  563.6 2.9 fusion.2
Async XLA Ops:
  550.3 4.2 copy-start.2
  559.5 4.1 copy-start
  559.5 4.1 copy-start.1
  559.5 4.1 copy-start.3
  559.5 4.1 copy-start.4
  559.5 4.1 copy-start.5
  559.6 4.1 copy-start.6

commit v2 on v0

v2 whole, which is shorter than its diff:
```python
import functools
import itertools
import math

import jax
import jax.numpy as jnp
from jax import lax
from jax.experimental import pallas as pl
from jax.experimental.pallas import tpu as pltpu
from jax.sharding import PartitionSpec as P

F32, BF16 = jnp.float32, jnp.bfloat16
MESH = pl.DeviceIdType.MESH
ANY = pl.BlockSpec(memory_space=pl.ANY)
VMEM_LIMIT = 63 * 1024 * 1024
LANES = 128
SUB_ROWS, SUB_COLS, SLICE = 512, 256, 32


def dot(a, b):
    return jnp.dot(a, b, preferred_element_type=F32)


def dot_t(a, b):
    return lax.dot_general(a, b, (((1,), (1,)), ((), ())), preferred_element_type=F32)


def aligned(start, size):
    return pl.ds(pl.multiple_of(start, size), size)


def div(a, b):
    return lax.div(a, jnp.int32(b))


def rem(a, b):
    return lax.rem(a, jnp.int32(b))


def where(test, a, b):
    return lax.select(test, jnp.asarray(a, jnp.int32), jnp.asarray(b, jnp.int32))


def normed(h):
    wide = h.astype(F32)
    return (wide * lax.rsqrt(jnp.mean(wide * wide, -1, keepdims=True) + 1e-6)).astype(BF16)


def normed_back(h, by_a):
    wide = h.astype(F32)
    scale = lax.rsqrt(jnp.mean(wide * wide, -1, keepdims=True) + 1e-6)
    inner = jnp.mean(by_a * wide, -1, keepdims=True)
    return (by_a * scale - wide * (scale * scale * scale * inner)).astype(BF16)


class Place:
    def __init__(self, n):
        self.side = math.isqrt(n // 2)
        assert self.side == 4 and self.side * self.side * 2 == n, n
        self.me = lax.axis_index("dp")
        self.k = rem(self.me, 2)
        chip = div(self.me, 2)
        x, y = div(chip, self.side), rem(chip, self.side)
        self.pa = where(self.k == 0, x, y)
        self.pb = where(self.k == 0, y, x)
        self.partner = chip * 2 + 1 - self.k
        self.x, self.y = x, y
        self.near = self.core(1, 0), self.core(-1, 0), self.core(0, 1), self.core(0, -1), self.partner

    def lines(self):
        side, row = self.side, 2 * self.side
        spot = self.x * 2 + self.k

        def along_x(i):
            i = rem(spot + i, row)
            return (div(i, 2) * side + self.y) * 2 + rem(i, 2)

        def along_y(i):
            return (self.x * side + rem(self.y + i, side)) * 2 + self.k

        return (spot, row, along_x), (self.y, side, along_y)

    def spot(self, a, b):
        a, b = rem(self.pa + a + self.side, self.side), rem(self.pb + b + self.side, self.side)
        return where(self.k == 0, a, b), where(self.k == 0, b, a)

    def chip(self, a, b):
        a, b = rem(self.pa + a + self.side, self.side), rem(self.pb + b + self.side, self.side)
        return self.at(a, b)

    def at(self, a, b):
        return where(self.k == 0, a * self.side + b, b * self.side + a)

    def core(self, a, b):
        return self.chip(a, b) * 2 + self.k

    def neighbours(self):
        return self.near


def greet(others):
    barrier = pltpu.get_barrier_semaphore()
    for other in others:
        pl.semaphore_signal(barrier, inc=1, device_id={"dp": other}, device_id_type=MESH)
    pl.semaphore_wait(barrier, len(others))


def remote(src, dst, send, recv, other):
    return pltpu.make_async_remote_copy(
        src_ref=src, dst_ref=dst, send_sem=send, recv_sem=recv, device_id={"dp": other}, device_id_type=MESH
    )


def gather_tick(place, tau, total, sems, own, buf):
    own_sem, send, recv = sems
    up_a, down_a, up_b, down_b, partner = place.neighbours()
    k = place.k
    half = own.shape[1] // 2
    low, high = pl.ds(0, half), pl.ds(half, half)
    slots = own_sem.shape[0]

    def stage(number, body):
        n = tau - 2 * number
        pl.when((n >= 0) & (n < total))(lambda: body(n, rem(n, slots)))

    def two(n, s, base, src_up, src_down, up, down):
        return (
            remote(src_up, src_up, send.at[s, base], recv.at[s, base], up),
            remote(src_down, src_down, send.at[s, base + 1], recv.at[s, base + 1], down),
        )

    def at(n, a, b, *rows):
        x, y = place.spot(a, b)
        return buf.at[(n, x, y, k) + rows]

    def own_copies(n, s):
        src, dst = own.at[n], at(n, 0, 0)
        return (
            remote(src, dst, send.at[s, 0], recv.at[s, 0], up_a),
            remote(src, dst, send.at[s, 1], recv.at[s, 1], down_a),
        )

    def along_a(n, s):
        return two(n, s, 2, at(n, -1, 0, low), at(n, 1, 0, high), up_a, down_a)

    def lines(n, b, rows=slice(None)):
        x, y = place.spot(0, b)
        yield from (buf.at[n, :, y, 0, rows], buf.at[n, x, :, 1, rows])

    def start_lines(s, base, ups, downs):
        for core, (src_up, src_down) in enumerate(zip(ups, downs, strict=True)):

            @pl.when(k == core)
            def _():
                for cp in two(None, s, base, src_up, src_down, up_b, down_b):
                    cp.start()

    def across(n, s):
        plane = buf.at[n, :, :, k]
        return remote(plane, plane, send.at[s, 8], recv.at[s, 8], partner)

    def wait_both(n, s, base, size):
        for d in range(2):
            for sem in (send, recv):
                pltpu.make_async_copy(size(n), size(n), sem.at[s, base + d]).wait()

    one = lambda n: buf.at[n, 0, 0, 0]
    one_half = lambda n: buf.at[n, 0, 0, 0, low]
    four = lambda n: buf.at[n, 0, :, 0]
    four_half = lambda n: buf.at[n, 0, :, 0, low]

    def stage0(n, s):
        for cp in own_copies(n, s):
            cp.start()
        pltpu.make_async_copy(own.at[n], at(n, 0, 0), own_sem.at[s]).start()

    def stage1(n, s):
        wait_both(n, s, 0, one)
        for cp in along_a(n, s):
            cp.start()
        pltpu.make_async_copy(own.at[n], at(n, 0, 0), own_sem.at[s]).wait()

    def stage2(n, s):
        wait_both(n, s, 2, one_half)
        start_lines(s, 4, lines(n, 0), lines(n, 0))

    def stage3(n, s):
        wait_both(n, s, 4, four)
        start_lines(s, 6, lines(n, -1, low), lines(n, 1, high))

    def stage4(n, s):
        wait_both(n, s, 6, four_half)
        across(n, s).start()

    def stage5(n, s):
        across(n, s).wait()

    for number, body in enumerate((stage0, stage1, stage2, stage3, stage4, stage5)):
        stage(number, body)


GATHER_DEPTH = 10


def step_kernel(
    n_dev, x_h, dy_h, wg_h, wu_h, wd_h,
    buf_h, p_h, grads_h, fin_h, total_o,
    own, h, a, by, acc, guv,
    byT, grad, got0, out1, got1, out2, got2, mid, out3, got3, out4, got4, fin, squares, rows1, rows2,
    own_sem, g_send, g_recv, in_sem, gu_sem, wd_sem, p_sem, dout_sem,
    load_sem, s_send, s_recv, fin_sem, credit, sum_send, sum_recv,
):
    place = Place(n_dev)
    layers, rows_g, ff = wg_h.shape
    rows_d = wd_h.shape[1]
    tokens, d = x_h.shape
    blocks, quarters, strip = 2, 4, 256
    chips = n_dev // 2
    unit_rows, gu = own.shape[1:]
    per = gu // LANES
    units = ff // gu
    downs = rows_d // unit_rows
    halves = rows_d // LANES
    per_half, per_down = units // halves, downs // halves
    unit = (chips, 2, unit_rows, gu)
    pairs = place.side * 2 // per
    assert halves == 2 and units == 2 * downs and layers == 2
    total = units + downs

    def split(u):
        return div(u, per_half), rem(u, per_half)

    def at_gu(layer, u):
        half_no, i = split(u)
        return layer * total + half_no * (per_half + per_down) + (layer * per_down) + i

    def at_down(layer, q):
        half_no, i = div(q, per_down), rem(q, per_down)
        return layer * total + half_no * (per_half + per_down) + ((1 - layer) * per_half) + i

    def own_pieces(layer, u, sem):
        half_no, group = split(u)
        n = at_gu(layer, u)
        for j in range(per):
            cols = aligned((group * per + j) * rows_d + half_no * LANES, LANES)
            for w, r in ((wg_h, 0), (wu_h, rows_g)):
                yield pltpu.make_async_copy(
                    w.at[layer, :, cols], own.at[n, pl.ds(r, rows_g), pl.ds(j * LANES, LANES)], in_sem.at[sem]
                )

    def own_down(layer, q, sem):
        return pltpu.make_async_copy(wd_h.at[layer, aligned(q * unit_rows, unit_rows)], own.at[at_down(layer, q)], in_sem.at[sem])

    early = 4

    @pl.loop(0, early)
    def _(u):
        for cp in own_pieces(0, u, 2):
            cp.start()

    loads = [(x_h, h), (dy_h, by)]
    for i, (src, dst) in enumerate(loads):
        pltpu.make_async_copy(src, dst, in_sem.at[i]).start()

    lines = place.lines()
    greet([other(i) for _, length, other in lines for i in range(1, length)])
    pltpu.make_async_copy(own.at[pl.ds(0, early)], own.at[pl.ds(0, early)], in_sem.at[2]).wait()

    def gather(tau):
        gather_tick(place, tau, layers * total, (own_sem, g_send, g_recv), own, buf_h)

    def gathers(first, count):
        @pl.loop(0, count)
        def _(i):
            gather(first + i)

    gathers(0, 2)
    for layer in range(layers):

        @pl.loop(early if layer == 0 else 0, units)
        def _(u):
            for cp in own_pieces(layer, u, 3):
                cp.start()

        @pl.loop(0, downs)
        def _(q):
            own_down(layer, q, 3).start()

    for i, (src, dst) in enumerate(loads):
        pltpu.make_async_copy(src, dst, in_sem.at[i]).wait()

    @pl.loop(0, tokens // strip)
    def _(t):
        rows = aligned(t * strip, strip)
        a[rows] = normed(h[rows])
        acc[rows] = jnp.zeros((strip, d), F32)

    squares[...] = jnp.zeros_like(squares)
    rest = own.at[pl.ds(early, layers * total - early)]
    pltpu.make_async_copy(rest, rest, in_sem.at[3]).wait()
    strips = tokens // strip

    def gu_load(n, slot):
        return pltpu.make_async_copy(buf_h.at[n], guv.at[slot], gu_sem.at[slot])

    def gate_up(slot):
        w = guv[slot].reshape(n_dev, unit_rows, gu)
        return w[:, :rows_g].reshape(d, gu), w[:, rows_g:].reshape(d, gu)

    def forward(pbuf, wdv):
        slots = pbuf.shape[0]

        def wd_load(q):
            part = rem(q, per_down)
            return pltpu.make_async_copy(
                buf_h.at[at_down(0, q)], wdv.at[:, :, :, aligned(part * unit_rows, unit_rows)], wd_sem.at[0, part]
            )

        def p_store(u):
            slot = rem(u, slots)
            return pltpu.make_async_copy(pbuf.at[slot], p_h.at[u], p_sem.at[slot])

        def hidden(u):
            slot, out = rem(u, 2), rem(u, slots)
            gu_load(at_gu(0, u), slot).wait()
            pl.when(u >= slots)(lambda: p_store(u - slots).wait())

            @pl.loop(0, blocks)
            def _(t):
                tb = tokens // blocks
                wg, wu = gate_up(slot)
                for r in range(0, tb, SUB_ROWS):
                    at = a[aligned(t * tb + r, SUB_ROWS)]
                    for col in range(0, gu, SUB_COLS):
                        cols = slice(col, col + SUB_COLS)
                        g_all, up_all = dot(at, wg[:, cols]), dot(at, wu[:, cols])
                        for q in range(0, SUB_ROWS, SLICE):
                            g, up = g_all[q : q + SLICE], up_all[q : q + SLICE]
                            hid = g * (1.0 / (1.0 + jnp.exp(-g))) * up
                            pbuf[out, aligned(t * tb + r + q, SLICE), cols] = hid.astype(BF16)

            p_store(u).start()

        @pl.loop(2, GATHER_DEPTH + 1)
        def _(tau):
            gather(tau)
            pl.when(tau == GATHER_DEPTH)(lambda: gu_load(0, 0).start())

            @pl.when(tau < 2 + strips)
            def _():
                rows = aligned((tau - 2) * strip, strip)
                byT[:, rows] = by[rows].astype(F32).T.astype(BF16)

        @pl.loop(0, halves)
        def _(half_no):
            now = GATHER_DEPTH + 1 + half_no * (per_half + per_down - 1 + quarters)

            @pl.loop(0, per_half)
            def _(i):
                gather(now + i)
                u = half_no * per_half + i

                @pl.when(i + 1 < per_half)
                def _():
                    gu_load(at_gu(0, u + 1), rem(u + 1, 2)).start()

                q = i - per_half + per_down

                @pl.when((q >= 0) & (half_no == 1))
                def _():
                    wd_load(per_down + q).start()

                hidden(u)

            now += per_half

            @pl.when(half_no == 0)
            def _():
                @pl.loop(0, per_down)
                def _(q):
                    pl.when(q > 0)(lambda: gather(now + q - 1))
                    wd_load(q).start()

            now += where(half_no == 0, per_down - 1, 0)
            for q in range(per_down):
                wd_load(jnp.int32(q)).wait()

            @pl.loop(0, quarters)
            def _(t):
                gather(now + t)

                @pl.when((t == quarters - 1) & (half_no == 0))
                def _():
                    gu_load(at_gu(0, per_half), 0).start()

                rows = aligned(t * (tokens // quarters), tokens // quarters)
                result = acc[rows]
                for j in range(per_half):
                    w = wdv[j // pairs, pl.ds(j % pairs * (per // 2), per // 2)].reshape(gu, d)
                    result += dot(pbuf[j, rows], w)
                acc[rows] = result

        for i in range(slots):
            p_store(jnp.int32(units - slots + i)).wait()

    pl.run_scoped(
        forward,
        pltpu.VMEM((per_half, tokens, gu), BF16),
        pltpu.VMEM((place.side, place.side, 2, LANES, d), BF16),
    )
    after = GATHER_DEPTH + 1 + per_half + (per_down - 1) + quarters + per_half + quarters

    gathers(after, 2)
    after += 2

    phase1 = blocks * (units + 1)
    phase2 = phase1 + 2
    phase3 = phase2 + units // 2
    made = 2 * blocks - 1
    early_down = blocks * (per_half + 2)
    later = downs - per_down
    last_tick = phase3 + made + 2 * (units - 1)
    windows = (
        ((early_down, early_down + 2 * per_down), (phase2, phase3 + 2 * downs)),
        ((made, made + 2 * units), (phase3 + made, last_tick + 2)),
    )
    assert blocks == 2 and phase3 == phase2 + 2 * later and phase3 % 2 == 0 and early_down % 2 == 0 and made % 2 == 1

    assert last_tick == phase3 + blocks * (units + 1) - 1

    def number(tau, odd):
        pair = where(tau < phase2, total + div(tau - made, 2), div(tau - phase3 - made, 2))
        down = where(tau < phase3, total + units + per_down + div(tau - phase2, 2), units + div(tau - phase3, 2))
        down = where(tau < phase2, total + units + div(tau - early_down, 2), down)
        return where(odd == 1, pair, down)

    scatter = Scatter(
        place, windows, number, grads_h, fin_h,
        (grad, got0, out1, got1, out2, got2, mid, out3, got3, out4, got4, fin, squares, load_sem, s_send, s_recv, fin_sem, credit),
    )

    def backward(aT, hid, wdc, dout):
        ps, dg, du = (hid.at[pl.ds(2 * i, 2)] for i in range(3))

        def weights_of(layer, u, slot):
            half_no, group = split(u)
            yield gu_load(at_gu(layer, u), slot)
            for part in range(per_down):
                yield pltpu.make_async_copy(
                    buf_h.at[at_down(layer, half_no * per_down + part), div(group, pairs), aligned(rem(group, pairs) * (per // 2), per // 2)],
                    wdc.at[slot, :, :, pl.ds(part * unit_rows, unit_rows)],
                    wd_sem.at[slot, part],
                )

        def down_store(layer, c, slots=2):
            slot = rem(c, slots)
            half_no, group = split(c)
            for part in range(per_down):
                yield pltpu.make_async_copy(
                    dout.at[slot, :, :, pl.ds(part * unit_rows, unit_rows)],
                    grads_h.at[layer * total + units + half_no * per_down + part, aligned(group * (per // 2), per // 2)],
                    dout_sem.at[slot, part],
                )

        def made_in(layer, c):
            return rem((0 if layer else phase3) + blocks * c + blocks - 1, grad.shape[0])

        def body(layer, c, t, now, before, grads, sums):
            top = layer == layers - 1
            backward_body(
                c, t, now, before, grads, blocks, a, aT, by, byT, acc if top else None, ps if top else None, dg, du,
                gate_up, lambda slot: wdc[slot].reshape(gu, d), grad.at[made_in(layer, c)], dout if top else None, sums,
            )

        first, last = jnp.int32(0), jnp.int32(units)
        for cp in weights_of(1, first, first):
            cp.start()

        @pl.loop(0, tokens // strip)
        def _(t):
            rows = aligned(t * strip, strip)
            h1 = (h[rows].astype(F32) + acc[rows].astype(BF16).astype(F32)).astype(BF16)
            h[rows] = h1
            a1 = normed(h1)
            a[rows] = a1
            aT[:, rows] = a1.astype(F32).T.astype(BF16)

        def clear():
            acc[...] = jnp.zeros_like(acc)

        def ticked1(c, t, work):
            if c is last:
                scatter.around(blocks * c + t, work)
                return

            @pl.when((t == 0) & (after + 2 * c < layers * total + GATHER_DEPTH))
            def _():
                gathers(after + 2 * c, 2)

            scatter.around(blocks * c + t, work)

        backward_loop(units, blocks, last, functools.partial(body, 1), functools.partial(weights_of, 1), functools.partial(down_store, 1), ticked1, clear)

        cp_x = pltpu.make_async_copy(x_h, a, in_sem.at[0])
        cp_x.start()

        def p_loads(i):
            for j in range(2):
                slot = 2 * rem(i, 2) + j
                yield pltpu.make_async_copy(p_h.at[2 * i + j], hid.at[slot], p_sem.at[slot])

        def down_stores(i):
            for j in range(2):
                yield from down_store(0, 2 * i + j, 4)

        for cp in itertools.chain(p_loads(first), weights_of(0, first, first)):
            cp.start()
        scatter.tick(jnp.int32(phase1))
        cp_x.wait()

        @pl.loop(0, tokens // strip)
        def _(t):
            rows = aligned(t * strip, strip)
            back = normed_back(h[rows], acc[rows].astype(BF16).astype(F32))
            by1 = (by[rows].astype(F32) + back.astype(F32)).astype(BF16)
            by[rows] = by1
            byT[:, rows] = by1.astype(F32).T.astype(BF16)
            a0 = normed(a[rows])
            a[rows] = a0
            aT[:, rows] = a0.astype(F32).T.astype(BF16)

        scatter.tick(jnp.int32(phase1 + 1))

        @pl.loop(0, units // 2)
        def _(i):
            for cp in p_loads(i):
                cp.wait()

            @pl.when(2 * i + 2 < units)
            def _():
                for cp in p_loads(i + 1):
                    cp.start()

            @pl.when(i > 1)
            def _():
                for cp in down_stores(i - 2):
                    cp.wait()

            def work(sums):
                pieces = list(sums)
                for j in range(2):
                    slot = 2 * rem(i, 2) + j
                    for r in range(0, d, d // 2):
                        m = pl.ds(r, d // 2)
                        part = dot(byT[m], hid[slot])
                        for piece in pieces[:2]:
                            piece()
                        pieces = pieces[2:]
                        dout[slot, :, :, :, m] = part.T.astype(BF16).reshape(dout.shape[1:4] + (d // 2,))

            scatter.around(phase2 + i, work)
            for cp in down_stores(i):
                cp.start()

        for i in (units // 2 - 2, units // 2 - 1):
            for cp in down_stores(jnp.int32(i)):
                cp.wait()

        backward_loop(
            units, blocks, last, functools.partial(body, 0), functools.partial(weights_of, 0), lambda c: (),
            lambda c, t, work: scatter.around(phase3 + blocks * c + t, work),
        )
    pl.run_scoped(
        backward,
        pltpu.VMEM((d, tokens), BF16),
        pltpu.VMEM((6, tokens, gu), BF16),
        pltpu.VMEM((2, per // 2, 2, LANES, d), BF16),
        pltpu.VMEM((4, per // 2, 2, LANES, d), BF16),
    )

    scatter.at = DRAIN_AT
    scatter.allow(CREDIT)
    scatter.paced = False

    @pl.loop(0, len(DRAIN_AT) - 2)
    def _(i):
        scatter.tick(last_tick + 1 + 2 * i)

    scatter.when(last_tick + DRAIN_AT[7], 7, lambda b, s, began: scatter.store(s, 0).wait())

    so_far = jnp.full(rows1.shape[1:], jnp.sum(squares[...]), F32)
    for i, ((spot, length, other), rows) in enumerate(zip(lines, (rows1, rows2), strict=True)):
        rows[spot] = so_far
        cps = [remote(rows.at[spot], rows.at[spot], sum_send.at[i, j], sum_recv.at[i, spot], other(j)) for j in range(1, length)]
        for cp in cps:
            cp.start()
        for j in range(1, length):
            away = rem(spot + j, length)
            pltpu.make_async_copy(rows.at[away], rows.at[away], sum_recv.at[i, away]).wait()
        for cp in cps:
            cp.wait_send()
        so_far = rows[0]
        for j in range(1, length):
            so_far = so_far + rows[j]
    total_o[...] = so_far


def backward_body(c, t, now, before, grads, blocks, a, aT, by, byT, acc, ps, dg, du, gate_up, down, grad, dout, sums):
    slot = rem(c, 2)
    other = 1 - slot
    tokens, d = a.shape
    tb = tokens // blocks
    part = d // blocks
    fill = []

    def states(i):
        slot_b = where(t == 0, other, slot)
        rows_b = aligned(rem(t + blocks - 1, blocks) * tb + i * (tb // 2), tb // 2)
        wg, wu = gate_up(slot_b)
        acc[rows_b] += dot_t(dg[slot_b, rows_b], wg) + dot_t(du[slot_b, rows_b], wu)

    def weights(i):
        m = aligned(t * part, part)
        if i == 2:
            dout[other, :, :, :, m] = dot(byT[m], ps[other]).T.astype(BF16).reshape(dout.shape[1:4] + (part,))
            return
        rows_g = grad.shape[2] // 2
        chips = part // rows_g // 2
        value = dot(aT[m], (dg, du)[i][other]).astype(BF16)
        grad[aligned(t * chips, chips), :, pl.ds(i * rows_g, rows_g)] = value.reshape(chips, 2, rows_g, -1)

    if before and acc is not None:
        fill += [functools.partial(states, i) for i in range(2)]
    if grads:
        fill += [functools.partial(weights, i) for i in range(3 if ps is not None else 2)]
    if sums is not None:
        fill = [piece for pair in itertools.zip_longest(fill, sums) for piece in pair if piece is not None]
    if not now:
        for piece in fill:
            piece()
        return
    wg, wu = gate_up(slot)
    wd = down(slot)
    gu = wg.shape[1]
    tiles = [(r, col) for r in range(0, tb, SUB_ROWS) for col in range(0, gu, SUB_COLS)]
    done = 0
    for i, (r, col) in enumerate(tiles):
        cols = slice(col, col + SUB_COLS)
        rows = aligned(t * tb + r, SUB_ROWS)
        at = a[rows]
        g_all, up_all = dot(at, wg[:, cols]), dot(at, wu[:, cols])
        dp_all = dot_t(by[rows], wd[cols])
        while done < len(fill) * (i + 1) // len(tiles):
            fill[done]()
            done += 1
        for q in range(0, SUB_ROWS, SLICE):
            g, up, dp = g_all[q : q + SLICE], up_all[q : q + SLICE], dp_all[q : q + SLICE].astype(BF16).astype(F32)
            sig = 1.0 / (1.0 + jnp.exp(-g))
            silu = g * sig
            out = aligned(t * tb + r + q, SLICE)
            if ps is not None:
                ps[slot, out, cols] = (silu * up).astype(BF16)
            du[slot, out, cols] = (dp * silu).astype(BF16)
            dg[slot, out, cols] = (dp * up * (sig + silu * (1.0 - sig))).astype(BF16)


def backward_loop(units, blocks, last, body, weights_of, flush, ticked, first_body_done=None):
    zero = jnp.int32(0)

    def each(c, action, copies):
        for cp in copies(c):
            getattr(cp, action)()

    def weights(c):
        return weights_of(c, rem(c, 2))

    each(zero, "wait", weights)

    @pl.loop(0, blocks)
    def _(t):
        ticked(zero, t, lambda sums: body(zero, t, True, True, False, sums))

        @pl.when(t == 0)
        def _():
            each(jnp.int32(1), "start", weights)
            if first_body_done is not None:
                first_body_done()

    @pl.loop(blocks, units * blocks)
    def _(i):
        c, t = div(i, blocks), rem(i, blocks)
        pl.when(t == 0)(lambda: each(c, "wait", weights))
        ticked(c, t, lambda sums: body(c, t, True, True, True, sums))

        @pl.when(t == 0)
        def _():
            pl.when(c + 1 < units)(lambda: each(c + 1, "start", weights))
            pl.when(c > 1)(lambda: each(c - 2, "wait", flush))

        pl.when(t == blocks - 1)(lambda: each(c - 1, "start", flush))

    body(last, zero, False, True, False, None)

    @pl.loop(0, blocks)
    def _(t):
        ticked(last, t, lambda sums: body(last, t, False, False, True, sums))
        pl.when(t == 0)(lambda: each(last - 2, "wait", flush))

    each(last - 1, "start", flush)
    each(last - 1, "wait", flush)


SCATTER_AT = (0, 1, 3, 6, 8, 10, 12, 13)
DRAIN_AT = (0, 1, 3, 5, 7, 9, 11, 13)
CREDIT = 3


class Scatter:
    def __init__(self, place, windows, number, source, target, refs):
        self.place, self.windows, self.number, self.source, self.target = place, windows, number, source, target
        (self.grad, self.got0, self.out1, self.got1, self.out2, self.got2, self.mid, self.out3, self.got3, self.out4, self.got4,
         self.fin, self.squares, self.load_sem, self.send, self.recv, self.fin_sem, self.credit) = refs
        self.half = self.grad.shape[3] // 2
        self.at, self.paced, self.now = SCATTER_AT, True, None

    def slots(self, tau, stage):
        began = tau - self.at[stage] + 2 * self.grad.shape[0] * self.send.shape[0]
        return rem(began, self.grad.shape[0]), rem(began, self.send.shape[0])

    def bounds(self, tau):
        odd = rem(tau, 2) == 1
        return [
            [[where(odd, *(pair if same else pair[::-1])) for pair in zip(o, e, strict=True)] for e, o in zip(*self.windows, strict=True)]
            for same in (True, False)
        ]

    def here(self, tau, stage):
        if self.now is not tau:
            self.now, self.found, self.limits = tau, {}, self.bounds(tau)
        began = tau - self.at[stage]
        (low0, high0), (low1, high1) = self.limits[self.at[stage] % 2]
        if stage not in self.found:
            self.found[stage] = ((began >= low0) & (began < high0)) | ((began >= low1) & (began < high1))
        return self.found[stage]

    def when(self, tau, stage, body):
        b, s = self.slots(tau, stage)
        began = tau - self.at[stage]
        pl.when(self.here(tau, stage))(lambda: body(b, s, began))

    def which(self, began):
        return self.number(began, rem(began, 2))

    def load(self, b, n):
        return pltpu.make_async_copy(self.source.at[n], self.grad.at[b], self.load_sem.at[b])

    def store(self, s, n):
        return pltpu.make_async_copy(self.fin.at[s], self.target.at[n], self.fin_sem.at[s])

    def copies(self, stage, b, s):
        up_a, down_a, up_b, down_b, partner = self.place.neighbours()
        if stage == 1:
            src = self.grad.at[b, :, 1 - self.place.k]
            return (remote(src, self.got0.at[b], self.send.at[s, 0], self.recv.at[s, 0], partner),)
        out, got, base, up, down = (
            (self.out1, self.got1, 1, up_b, down_b),
            (self.out2, self.got2, 3, up_b, down_b),
            (self.out3, self.got3, 5, up_a, down_a),
            (self.out4, self.got4, 7, up_a, down_a),
        )[stage - 2]
        return tuple(
            remote(out.at[s, i], got.at[s, i], self.send.at[s, base + i], self.recv.at[s, base + i], other)
            for i, other in enumerate((up, down))
        )

    def allow(self, ticks):
        for i in range(len(self.place.neighbours())):
            pl.semaphore_wait(self.credit.at[i], ticks)

    def before(self, tau):
        if self.paced:
            pl.when(tau >= CREDIT)(lambda: self.allow(1))

        def down_only(action):
            def body(b, s, began):
                pl.when(rem(began, 2) == 0)(lambda: action(b, began))

            return body

        self.when(tau, 0, down_only(lambda b, began: self.load(b, self.which(began)).start()))

        def across(b, s, began):
            down_only(lambda b, began: self.load(b, 0).wait())(b, s, began)
            for cp in self.copies(1, b, s):
                cp.start()

        self.when(tau, 1, across)
        for stage in range(2, 7):

            def arrived(b, s, began, stage=stage):
                for cp in self.copies(stage - 1, b, s):
                    cp.wait()

            self.when(tau, stage, arrived)
        self.when(tau, 7, lambda b, s, began: self.store(s, 0).wait())

    def after(self, tau):
        for stage in range(2, 6):

            def go(b, s, began, stage=stage):
                for cp in self.copies(stage, b, s):
                    cp.start()

            self.when(tau, stage, go)
        self.when(tau, 6, lambda b, s, began: self.store(s, self.which(began)).start())
        for other, seen_as in zip(self.place.neighbours(), (1, 0, 3, 2, 4), strict=True) if self.paced else ():
            pl.semaphore_signal(self.credit.at[seen_as], inc=1, device_id={"dp": other}, device_id_type=MESH)

    def sums(self, tau):
        return [functools.partial(getattr(self, f"sum{stage}"), tau) for stage in range(2, 7)]

    def mine(self, b, i, step):
        chip = self.place.at(i, rem(self.place.pb + step, self.place.side))
        return self.grad[b, chip, self.place.k].astype(F32) + self.got0[b, chip].astype(F32)

    def sum2(self, tau):
        b, s = self.slots(tau, 2)
        for i in range(self.place.side):
            total = self.mine(b, i, 2)
            self.out1[s, 0, i] = total[: self.half].astype(BF16)
            self.out1[s, 1, i] = total[self.half :].astype(BF16)

    def add_half(self, out, index, way, total, got):
        half = self.half
        whole, rest = slice(half * way, half * way + half), slice(half * (1 - way), half * (2 - way))
        out[index + (pl.ds(half * way, half),)] = (total[whole] + got.astype(F32)).astype(BF16)
        out[index + (pl.ds(half * (1 - way), half),)] = total[rest].astype(BF16)

    def sum3(self, tau):
        b, s = self.slots(tau, 3)
        for i in range(self.place.side):
            for way, step in ((0, 1), (1, self.place.side - 1)):
                self.add_half(self.out2, (s, way, i), way, self.mine(b, i, step), self.got1[s, way, i])

    def sum4(self, tau):
        b, s = self.slots(tau, 4)
        for i in range(self.place.side):
            self.mid[b, i] = self.mine(b, i, 0) + self.got2[s, 0, i].astype(F32) + self.got2[s, 1, i].astype(F32)
        far = self.mid[b, rem(self.place.pa + 2, self.place.side)]
        self.out3[s, 0] = far[: self.half].astype(BF16)
        self.out3[s, 1] = far[self.half :].astype(BF16)

    def sum5(self, tau):
        b, s = self.slots(tau, 5)
        for way, step in ((0, 1), (1, self.place.side - 1)):
            total = self.mid[b, rem(self.place.pa + step, self.place.side)]
            self.add_half(self.out4, (s, way), way, total, self.got3[s, way])

    def sum6(self, tau):
        b, s = self.slots(tau, 6)
        total = self.mid[b, self.place.pa] + self.got4[s, 0].astype(F32) + self.got4[s, 1].astype(F32)
        result = total.astype(BF16)
        self.fin[s] = result
        here = self.here(tau, 6)
        squared = result.astype(F32) * result.astype(F32)
        self.squares[...] += jnp.where(here, squared, 0.0)

    def tick(self, tau):
        self.before(tau)
        for piece in self.sums(tau):
            piece()
        self.after(tau)

    def around(self, tau, work):
        self.before(tau)
        work(self.sums(tau))
        self.after(tau)


def adamw(w, m, v, g):
    w = w.astype(F32)
    m = 0.9 * m + 0.1 * g
    v = 0.95 * v + 0.05 * g * g
    step = m * lax.rsqrt(v + 1e-8) + 0.1 * w
    return (w - 0.02 * step).astype(BF16), m, v


def update_kernel(count, squares, pair0, pair1, down, *refs):
    ins, outs = refs[:9], refs[9:]
    factor = jnp.minimum(1.0, 0.5 * lax.rsqrt(squares[0:1, 0:1] / count + 1e-30))
    rows_g = ins[0].shape[1]
    some, unit_rows, gu = pair0.shape[1:]

    def update(i, where, g):
        new = adamw(*(ref[where] for ref in ins[i::3]), g.astype(F32) * factor)
        for ref, value in zip(outs[i::3], new, strict=True):
            ref[where] = value

    for p in range(some):
        for i in range(2):
            rows = slice(i * rows_g, (i + 1) * rows_g)
            g = [half[0, p, rows, c : c + LANES] for c in range(0, gu, LANES) for half in (pair0, pair1)]
            update(i, (0, slice(None), pl.ds(p * 2 * gu, 2 * gu)), jnp.concatenate(g, 1))
        update(2, (0, pl.ds(p * unit_rows, unit_rows)), down[0, p])


def solution(mesh):
    n_dev = mesh.shape["dp"]

    def step(x, dy, *arrays):
        weights, m, v = (arrays[i : i + 3] for i in (0, 3, 6))
        x, dy = x[0], dy[0]
        w_gate, w_up, w_down = weights
        layers, rows_g, ff = w_gate.shape
        assert layers == 2
        rows_d, d = w_down.shape[1:]
        tokens = x.shape[0]
        chips = n_dev // 2
        halves = rows_d // LANES
        gu = d
        units, unit_rows = ff // gu, 2 * rows_g
        downs = rows_d // unit_rows
        per = gu // LANES
        total = units + downs
        vmem, dma = pltpu.VMEM, pltpu.SemaphoreType.DMA
        shape = jax.ShapeDtypeStruct
        unit = (chips, 2, unit_rows, gu)
        states = (tokens, d)

        big, small, side = 10, 6, math.isqrt(chips)
        whole = (side, side) + unit[1:]
        half_block, block = (unit_rows // 2, gu), (unit_rows, gu)
        _, _, _, fin, squares = pl.pallas_call(
            functools.partial(step_kernel, n_dev),
            out_shape=(
                shape((layers * total,) + whole, BF16),
                shape((units, tokens, gu), BF16),
                shape((layers * total,) + unit, BF16),
                shape((layers * total,) + block, BF16),
                shape((8, LANES), F32),
            ),
            in_specs=[ANY] * 5,
            out_specs=[ANY] * 4 + [pl.BlockSpec(memory_space=vmem)],
            scratch_shapes=[
                vmem((layers * total,) + block, BF16),
                vmem(states, BF16),
                vmem(states, BF16),
                vmem(states, BF16),
                vmem(states, F32),
                vmem((2,) + whole, BF16),
                vmem(states[::-1], BF16),
                vmem((big,) + unit, BF16),
                vmem((big, chips) + block, BF16),
                vmem((small, 2, side) + half_block, BF16),
                vmem((small, 2, side) + half_block, BF16),
                vmem((small, 2, side) + block, BF16),
                vmem((small, 2, side) + block, BF16),
                vmem((big, side) + block, F32),
                vmem((small, 2) + half_block, BF16),
                vmem((small, 2) + half_block, BF16),
                vmem((small, 2) + block, BF16),
                vmem((small, 2) + block, BF16),
                vmem((small,) + block, BF16),
                vmem(block, F32),
                vmem((2 * side, 8, LANES), F32),
                vmem((side, 8, LANES), F32),
                dma((8,)),
                dma((8, 9)),
                dma((8, 9)),
                dma((4,)),
                dma((2,)),
                dma((2, downs // halves)),
                dma((units // halves,)),
                dma((4, downs // halves)),
                dma((big,)),
                dma((small, 9)),
                dma((small, 9)),
                dma((small,)),
                pltpu.SemaphoreType.REGULAR((5,)),
                dma((2, 2 * side)),
                dma((2, 2 * side)),
            ],
            compiler_params=pltpu.CompilerParams(collective_id=0, has_side_effects=True, vmem_limit_bytes=VMEM_LIMIT),
            name="step",
        )(x, dy, w_gate, w_up, w_down)
        fin = fin.reshape((layers, total) + block)
        some = 2
        steps = units // halves // some
        pair_block, down_block = (1, rows_g, some * halves * gu), (1, some * unit_rows, d)
        fins = [pl.BlockSpec((1, some) + block, lambda i, j, k=k: (i, k * steps + j, 0, 0)) for k in range(3)]
        each = [pl.BlockSpec(pair_block, lambda i, j: (i, 0, j))] * 2 + [pl.BlockSpec(down_block, lambda i, j: (i, j, 0))]
        kinds = [shape(w.shape, t) for t in (BF16, F32, F32) for w in weights]
        elements = layers * total * unit_rows * gu
        return pl.pallas_call(
            functools.partial(update_kernel, n_dev * elements),
            grid=(layers, steps),
            out_shape=kinds,
            in_specs=[pl.BlockSpec(squares.shape, lambda i, j: (0, 0))] + fins + each * 3,
            out_specs=each * 3,
            cost_estimate=pl.CostEstimate(flops=20 * elements, bytes_accessed=22 * elements, transcendentals=elements),
            name="update",
        )(squares, fin, fin, fin, *weights, *m, *v)

    states, cut = P(("rep", "dp"), None, None), P(None, "dp", None)
    return jax.shard_map(
        step,
        mesh=mesh,
        in_specs=(states, states) + (cut,) * 9,
        out_specs=(P("rep", "dp", None),) * 9,
        check_vma=False,
    )
```

time: 1080 us -> 544 us (0.50)
  matrix products: 571 us -> 0 us
  Pallas kernels: 0 us -> 543 us
  waiting for transfers between devices: 402 us -> 0 us
  blocking collectives: 46.5 us -> 0 us
  other arithmetic: 17.6 us -> 0 us
  between operations: 17.5 us -> 0.83 us
  local copies, waits for them, and re-layouts: 16.2 us -> 0 us
    dot_general x15 -> x0, matrix products: 571 us -> none  [the longest x5 217 us: layer(): gate = jnp.dot(a, w['w_gate'], preferred_element_type=jnp.float32)]
    pallas_call x0 -> x2, Pallas kernels: none -> 543 us  [the longest x1 534 us: step(): pl.pallas_call(functools.partial(step_kernel, n_dev), out_shape=(shape((l...]
    reduce_scatter x6 -> x0, waiting for transfers between devices: 282 us -> none  [step(): lax.psum_scatter(by_w[name], 'dp', scatter_dimension=0, tiled=True)]
    all_gather x6 -> x0, waiting for transfers between devices: 117 us -> none  [fetched(): lax.all_gather(w[number], 'dp', axis=0, tiled=True)]
    psum x1 -> x0, blocking collectives: 46.5 us -> none  [step(): squares = lax.psum(sum((jnp.sum(g * g) for g in gradients)), 'dp')]
  transfers between devices with their start and end apart: 12 -> 0, of which waited for: 9 -> 0; matrix products, arithmetic and copies ran while one was open for 39% -> 0% of each run, Pallas kernels for 0% -> 0%
where the time goes in v2:
time: 544 us
  Pallas kernels  543 us (100%)
    pallas_call x1, Pallas kernels, step(): pl.pallas_call(functools.partial(step_kernel, n_dev), out_shape=(shape((l...  534 us

profile of v2, /device:TPU:97, one launch (start us, length us, event | category | flops | bytes accessed | tf_op | source)
XLA Modules:
  0.0 543.7 jit_solution(8801317641924759234)
XLA Ops:
  0.6 533.8 %step.1 = (bf16[48,4,4,2,32,512]{5,4,3,2,1,0:T(8,128)(2,1)}, bf16[16,2048,512]{2,1,0:T(8,128)(2,1)}, bf16[48,16,2,32,512]{4,3,2,1,0:T(8,128)(2,1)}, bf16[48,32,512]{2,1,0:T(8,128)(2,1)}, f32[8,128]{1,0:T(8,128)}) custom-call(bf16[2048,512]{1,0:T(8,128)(2,1)} %bitcast.6, bf16[2048,512]{1,0:T(8,128)(2,1)} %bitcast.7, bf16[2,16,8192]{2,1,0:T(8,128)(2,1)} %refs_0_.1, ...), custom_call_target="tpu_custom_call" | custom-call | tf_op jit(solution)/shard_map/step/pallas_call | solution.py:933
  534.4 9.1 %update.1 = (bf16[2,16,8192]{2,1,0:T(8,128)(2,1)}, bf16[2,16,8192]{2,1,0:T(8,128)(2,1)}, bf16[2,256,512]{2,1,0:T(8,128)(2,1)}, f32[2,16,8192]{2,1,0:T(8,128)}, f...) custom-call(f32[8,128]{1,0:T(8,128)} %get-tuple-element.11.squares, ...), custom_call_target="tpu_custom_call" | custom-call | flops 15728640 | bytes 17301504 | tf_op jit(solution)/shard_map/update/pallas_call | solution.py:994

commit v3 on v2

--- a/solution.py
+++ b/solution.py
@@ -275,17 +275,18 @@
             gather(first + i)
 
     gathers(0, 2)
-    for layer in range(layers):
-
-        @pl.loop(early if layer == 0 else 0, units)
+
+    def own_loads(layer, start):
+        @pl.loop(start, units)
         def _(u):
-            for cp in own_pieces(layer, u, 3):
+            for cp in own_pieces(layer, u, 3 - layer):
                 cp.start()
 
         @pl.loop(0, downs)
         def _(q):
-            own_down(layer, q, 3).start()
-
+            own_down(layer, q, 3 - layer).start()
+
+    own_loads(0, early)
     for i, (src, dst) in enumerate(loads):
         pltpu.make_async_copy(src, dst, in_sem.at[i]).wait()
 
@@ -296,8 +297,9 @@
         acc[rows] = jnp.zeros((strip, d), F32)
 
     squares[...] = jnp.zeros_like(squares)
-    rest = own.at[pl.ds(early, layers * total - early)]
+    rest = own.at[pl.ds(early, total - early)]
     pltpu.make_async_copy(rest, rest, in_sem.at[3]).wait()
+    own_loads(1, 0)
     strips = tokens // strip
 
     def gu_load(n, slot):
@@ -351,6 +353,9 @@
                 rows = aligned((tau - 2) * strip, strip)
                 byT[:, rows] = by[rows].astype(F32).T.astype(BF16)
 
+        rest = own.at[pl.ds(total, total)]
+        pltpu.make_async_copy(rest, rest, in_sem.at[2]).wait()
+
         @pl.loop(0, halves)
         def _(half_no):
             now = GATHER_DEPTH + 1 + half_no * (per_half + per_down - 1 + quarters)
@@ -578,15 +583,12 @@
         pltpu.VMEM((4, per // 2, 2, LANES, d), BF16),
     )
 
-    scatter.at = DRAIN_AT
     scatter.allow(CREDIT)
     scatter.paced = False
 
-    @pl.loop(0, len(DRAIN_AT) - 2)
+    @pl.loop(0, SCATTER_AT[-1])
     def _(i):
-        scatter.tick(last_tick + 1 + 2 * i)
-
-    scatter.when(last_tick + DRAIN_AT[7], 7, lambda b, s, began: scatter.store(s, 0).wait())
+        scatter.tick(last_tick + 1 + i)
 
     so_far = jnp.full(rows1.shape[1:], jnp.sum(squares[...]), F32)
     for i, ((spot, length, other), rows) in enumerate(zip(lines, (rows1, rows2), strict=True)):
@@ -634,7 +636,7 @@
     if grads:
         fill += [functools.partial(weights, i) for i in range(3 if ps is not None else 2)]
     if sums is not None:
-        fill = [piece for pair in itertools.zip_longest(fill, sums) for piece in pair if piece is not None]
+        fill = [piece for pair in itertools.zip_longest(sums, fill) for piece in pair if piece is not None]
     if not now:
         for piece in fill:
             piece()
@@ -710,9 +712,8 @@
     each(last - 1, "wait", flush)
 
 
-SCATTER_AT = (0, 1, 3, 6, 8, 10, 12, 13)
-DRAIN_AT = (0, 1, 3, 5, 7, 9, 11, 13)
-CREDIT = 3
+SCATTER_AT = (0, 1, 3, 6, 9, 11, 13, 14)
+CREDIT = 2
 
 
 class Scatter:
@@ -817,7 +818,7 @@
             pl.semaphore_signal(self.credit.at[seen_as], inc=1, device_id={"dp": other}, device_id_type=MESH)
 
     def sums(self, tau):
-        return [functools.partial(getattr(self, f"sum{stage}"), tau) for stage in range(2, 7)]
+        return [functools.partial(getattr(self, f"sum{stage}"), tau) for stage in (4, 2, 3, 5, 6)]
 
     def mine(self, b, i, step):
         chip = self.place.at(i, rem(self.place.pb + step, self.place.side))

time: 544 us -> 525 us (0.965)
  Pallas kernels: 543 us -> 524 us
    pallas_call x1, Pallas kernels: 534 us -> 514 us  [step(): pl.pallas_call(functools.partial(step_kernel, n_dev), out_shape=(shape((l...]
where the time goes in v3:
time: 525 us; the launch traced here: 524 us
  Pallas kernels  524 us (100%)
    pallas_call x1, Pallas kernels, step(): pl.pallas_call(functools.partial(step_kernel, n_dev), out_shape=(shape((l...  514 us

profile of v3, /device:TPU:97, one launch (start us, length us, event | category | flops | bytes accessed | tf_op | source)
XLA Modules:
  0.0 524.4 jit_solution(7111399453521335156)
XLA Ops:
  0.6 514.5 %step.1 = (bf16[48,4,4,2,32,512]{5,4,3,2,1,0:T(8,128)(2,1)}, bf16[16,2048,512]{2,1,0:T(8,128)(2,1)}, bf16[48,16,2,32,512]{4,3,2,1,0:T(8,128)(2,1)}, bf16[48,32,512]{2,1,0:T(8,128)(2,1)}, f32[8,128]{1,0:T(8,128)}) custom-call(bf16[2048,512]{1,0:T(8,128)(2,1)} %bitcast.6, bf16[2048,512]{1,0:T(8,128)(2,1)} %bitcast.7, bf16[2,16,8192]{2,1,0:T(8,128)(2,1)} %refs_0_.1, ...), custom_call_target="tpu_custom_call" | custom-call | tf_op jit(solution)/shard_map/step/pallas_call | solution.py:934
  515.1 9.1 %update.1 = (bf16[2,16,8192]{2,1,0:T(8,128)(2,1)}, bf16[2,16,8192]{2,1,0:T(8,128)(2,1)}, bf16[2,256,512]{2,1,0:T(8,128)(2,1)}, f32[2,16,8192]{2,1,0:T(8,128)}, f...) custom-call(f32[8,128]{1,0:T(8,128)} %get-tuple-element.11.squares, ...), custom_call_target="tpu_custom_call" | custom-call | flops 15728640 | bytes 17301504 | tf_op jit(solution)/shard_map/update/pallas_call | solution.py:995
